TPU v7x, 512 devices: a whole 4x4x16 slice. The times are simulated.
512 devices in a mesh: gx: 8 (over y, z_hi), gy: 8 (over x, core), gz: 8 (over z_lo).
Axes of the slice: x: 4, y: 4, z: 16 (z_hi: 2, z_lo: 8; z = z_hi * 8 + z_lo), core: 2. Of those that a mesh axis runs over, the one named last changes fastest.
Arguments:
- weights: bfloat16 [2, 216, 262144], P(None, None, ('gx', 'gy', 'gz')), may hold values from -6 to 6
- translate: bfloat16 [2, 2, 216, 216], replicated, may hold values from -0.3125 to 0.3125
- angles: float32 [216, 256], replicated, may hold values from -3.140625 to 3.140625
- box_ids: int32 [9, 262144], P(None, ('gx', 'gy', 'gz')), may hold values from 0 to 255
Outputs:
- transformed: bfloat16 [2, 216, 262144], P(None, None, ('gx', 'gy', 'gz'))
All inputs are finite; a program needn't handle non-finite values.
Results may differ from a plain program's by a relative error of at most 0.018.
Values may be sent and summed in bfloat16 or wider, within the bound.
No kernel may reach another device: no remote copies, remote signals or barrier semaphores. Data moves between devices by JAX's collectives and lax.ppermute only.
A program may use at most 64 MiB of HBM per device.

v0:
```python
import jax
import jax.numpy as jnp
from jax import lax
from jax.sharding import PartitionSpec as P


def swapped(block, axis, apart):
    count = lax.axis_size(axis)
    route = []
    for low in range(count):
        high = low | 1 << apart
        if high != low and high < count:
            route += [(low, high), (high, low)]
    return lax.ppermute(block, axis, route)


def rotate(current, labels, cos_tab, sin_tab):
    cosines = jnp.take(cos_tab, labels, axis=1)
    sines = jnp.take(sin_tab, labels, axis=1)
    real_part = current[0].astype(jnp.float32)
    imag_part = current[1].astype(jnp.float32)
    return jnp.stack(
        [cosines * real_part - sines * imag_part, sines * real_part + cosines * imag_part]
    ).astype(jnp.bfloat16)


def combine(kept_half, received, translate, parity):
    own_mats = lax.dynamic_index_in_dim(translate, parity, 1, keepdims=False)
    far_mats = lax.dynamic_index_in_dim(translate, 1 - parity, 1, keepdims=False)
    halves = []
    for target in range(2):
        near_part = jnp.einsum(
            "jk,rkh->rjh", own_mats[target], kept_half, preferred_element_type=jnp.float32
        )
        far_part = jnp.einsum(
            "jk,rkh->rjh", far_mats[target], received, preferred_element_type=jnp.float32
        )
        halves.append(near_part + far_part)
    return jnp.concatenate(halves, axis=2).astype(jnp.bfloat16)


def run_swaps(current, box_ids, level_index, cos_tab, sin_tab, translate, position, extent, mover):
    for bit_no in range(extent.bit_length() - 1):
        rotated = rotate(current, box_ids[level_index], cos_tab, sin_tab)
        parity = jnp.right_shift(position, bit_no) & 1
        half_cols = rotated.shape[2] // 2
        kept_half = lax.dynamic_slice_in_dim(rotated, parity * half_cols, half_cols, 2)
        outgoing = lax.dynamic_slice_in_dim(rotated, (1 - parity) * half_cols, half_cols, 2)
        received = mover(outgoing, bit_no)
        current = combine(kept_half, received, translate, parity)
        level_index += 1
    return (current, level_index)


def shards(weights, translate, angles, box_ids):
    cos_tab = jnp.cos(angles)
    sin_tab = jnp.sin(angles)
    current = weights
    level_index = 0
    current, level_index = run_swaps(
        current,
        box_ids,
        level_index,
        cos_tab,
        sin_tab,
        translate,
        lax.axis_index("gx"),
        lax.axis_size("gx"),
        lambda parcel, which_bit: swapped(parcel, "gx", which_bit),
    )
    current, level_index = run_swaps(
        current,
        box_ids,
        level_index,
        cos_tab,
        sin_tab,
        translate,
        lax.axis_index("gy"),
        lax.axis_size("gy"),
        lambda parcel, which_bit: swapped(parcel, "gy", which_bit),
    )
    current, level_index = run_swaps(
        current,
        box_ids,
        level_index,
        cos_tab,
        sin_tab,
        translate,
        lax.axis_index("gz"),
        lax.axis_size("gz"),
        lambda parcel, which_bit: swapped(parcel, "gz", which_bit),
    )
    return current


def solution(mesh):
    in_specs = (P(None, None, ("gx", "gy", "gz")), P(), P(), P(None, ("gx", "gy", "gz")))
    out_specs = P(None, None, ("gx", "gy", "gz"))
    return jax.shard_map(shards, mesh=mesh, in_specs=in_specs, out_specs=out_specs, check_vma=False)
```

profile of v0, /device:TPU:1, one launch (start us, length us, event | category | flops | bytes accessed | tf_op | source)
XLA Modules:
  0.0 175.9 jit_solution(14842144227717053752)
XLA Ops:
  8.4 16.4 %collective-permute-start = (bf16[2,216,256]{2,1,0:T(8,128)(2,1)}, bf16[2,216,256]{2,1,0:T(8,128)(2,1)}, u32[]{:S(2)}, u32[]{:S(2)}) collective-permute-start(bf16[2,216,256]{2,1,0:T(8,128)(2,1)} %fusion.122), channel_id=1, source_target_pairs={{0,64},{64,0},{128,192},{192,128},{256,320},{320,256},{384,448},{4... | collective-permute-start | bytes 663560 | tf_op jit(solution)/shard_map/ppermute | solution.py:14
  31.2 2.2 %gather_fusion.5 = f32[512,216]{1,0:T(8,128)} fusion(f32[216,256]{0,1:T(8,128)S(1)} %get-tuple-element.24, s32[1024]{0:T(1024)S(1)} %pad_clamp_fusion.3), kind=kCustom, calls=%fused_computation.5.clone | custom fusion | bytes 886784 | tf_op jit(solution)/shard_map/jit(_take)/gather | solution.py:18
  33.5 2.2 %gather_fusion.12 = f32[512,216]{1,0:T(8,128)} fusion(f32[216,256]{0,1:T(8,128)S(1)} %get-tuple-element.25, s32[1024]{0:T(1024)S(1)} %pad_clamp_fusion.3), kind=kCustom, calls=%fused_computation.12.clone | custom fusion | bytes 886784 | tf_op jit(solution)/shard_map/jit(_take)/gather | solution.py:19
  35.7 2.2 %gather_fusion.4 = f32[512,216]{1,0:T(8,128)} fusion(f32[216,256]{0,1:T(8,128)S(1)} %get-tuple-element.24, s32[1024]{0:T(1024)S(1)} %pad_clamp_fusion.4), kind=kCustom, calls=%fused_computation.4.clone | custom fusion | bytes 886784 | tf_op jit(solution)/shard_map/jit(_take)/gather | solution.py:18
  40.2 2.2 %gather_fusion.14 = f32[512,216]{1,0:T(8,128)} fusion(f32[216,256]{0,1:T(8,128)S(1)} %get-tuple-element.25, s32[1024]{0:T(1024)S(1)} %pad_clamp_fusion.5), kind=kCustom, calls=%fused_computation.14.clone | custom fusion | bytes 886784 | tf_op jit(solution)/shard_map/jit(_take)/gather | solution.py:19
  44.7 2.2 %gather_fusion.15 = f32[512,216]{1,0:T(8,128)} fusion(f32[216,256]{0,1:T(8,128)S(1)} %get-tuple-element.25, s32[1024]{0:T(1024)S(1)} %pad_clamp_fusion.6), kind=kCustom, calls=%fused_computation.15.clone | custom fusion | bytes 886784 | tf_op jit(solution)/shard_map/jit(_take)/gather | solution.py:19
  49.2 2.2 %gather_fusion.16 = f32[512,216]{1,0:T(8,128)} fusion(f32[216,256]{0,1:T(8,128)S(1)} %get-tuple-element.25, s32[1024]{0:T(1024)S(1)} %pad_clamp_fusion.7), kind=kCustom, calls=%fused_computation.16.clone | custom fusion | bytes 886784 | tf_op jit(solution)/shard_map/jit(_take)/gather | solution.py:19
  51.4 2.2 %gather_fusion.1 = f32[512,216]{1,0:T(8,128)} fusion(f32[216,256]{0,1:T(8,128)S(1)} %get-tuple-element.24, s32[1024]{0:T(1024)S(1)} %pad_clamp_fusion.7), kind=kCustom, calls=%fused_computation.1.clone | custom fusion | bytes 886784 | tf_op jit(solution)/shard_map/jit(_take)/gather | solution.py:18
  53.7 2.2 %gather_fusion.17 = f32[512,216]{1,0:T(8,128)} fusion(f32[216,256]{0,1:T(8,128)S(1)} %get-tuple-element.25, s32[1024]{0:T(1024)S(1)} %pad_clamp_fusion.8), kind=kCustom, calls=%fused_computation.17.clone | custom fusion | bytes 886784 | tf_op jit(solution)/shard_map/jit(_take)/gather | solution.py:19
  79.3 3.4 %collective-permute-start.1 = (bf16[2,216,256]{2,1,0:T(8,128)(2,1)S(1)}, bf16[2,216,256]{2,1,0:T(8,128)(2,1)S(1)}, u32[]{:S(2)}, u32[]{:S(2)}) collective-permute-start(bf16[2,216,256]{2,1,0:T(8,128)(2,1)S(1)} %fusion.120), channel_id=1, source_target_pairs={{0,128},{128,0},{64,192},{192,64},{256,384},{384,256},{320,448},{4... | collective-permute-start | bytes 663560 | tf_op jit(solution)/shard_map/ppermute | solution.py:14
  83.2 4.0 %collective-permute-done.1 = bf16[2,216,256]{2,1,0:T(8,128)(2,1)S(1)} collective-permute-done((bf16[2,216,256]{2,1,0:T(8,128)(2,1)S(1)}, bf16[2,216,256]{2,1,0:T(8,128)(2,1)S(1)}, u32[]{:S(2)}, u32[]{:S(2)}) %collective-permute-start.1) | collective-permute-done | bytes 221216 | tf_op jit(solution)/shard_map/ppermute | solution.py:14
  88.8 4.8 %collective-permute-start.2 = (bf16[2,216,256]{2,1,0:T(8,128)(2,1)S(1)}, bf16[2,216,256]{2,1,0:T(8,128)(2,1)S(1)}, u32[]{:S(2)}, u32[]{:S(2)}) collective-permute-start(bf16[2,216,256]{2,1,0:T(8,128)(2,1)S(1)} %fusion.118), channel_id=1, source_target_pairs={{0,256},{256,0},{64,320},{320,64},{128,384},{384,128},{192,448},{4... | collective-permute-start | bytes 663560 | tf_op jit(solution)/shard_map/ppermute | solution.py:14
  94.1 3.3 %collective-permute-done.2 = bf16[2,216,256]{2,1,0:T(8,128)(2,1)S(1)} collective-permute-done((bf16[2,216,256]{2,1,0:T(8,128)(2,1)S(1)}, bf16[2,216,256]{2,1,0:T(8,128)(2,1)S(1)}, u32[]{:S(2)}, u32[]{:S(2)}) %collective-permute-start.2) | collective-permute-done | bytes 221216 | tf_op jit(solution)/shard_map/ppermute | solution.py:14
  99.0 4.6 %collective-permute-start.3 = (bf16[2,216,256]{2,1,0:T(8,128)(2,1)S(1)}, bf16[2,216,256]{2,1,0:T(8,128)(2,1)S(1)}, u32[]{:S(2)}, u32[]{:S(2)}) collective-permute-start(bf16[2,216,256]{2,1,0:T(8,128)(2,1)S(1)} %fusion.116), channel_id=1, source_target_pairs={{0,8},{8,0},{16,24},{24,16},{32,40},{40,32},{48,56},{56,48},{1,9},... | collective-permute-start | bytes 663560 | tf_op jit(solution)/shard_map/ppermute | solution.py:14
  106.3 3.1 %collective-permute-start.4 = (bf16[2,216,256]{2,1,0:T(8,128)(2,1)S(1)}, bf16[2,216,256]{2,1,0:T(8,128)(2,1)S(1)}, u32[]{:S(2)}, u32[]{:S(2)}) collective-permute-start(bf16[2,216,256]{2,1,0:T(8,128)(2,1)S(1)} %fusion.114), channel_id=1, source_target_pairs={{0,16},{16,0},{8,24},{24,8},{32,48},{48,32},{40,56},{56,40},{1,17}... | collective-permute-start | bytes 663560 | tf_op jit(solution)/shard_map/ppermute | solution.py:14
  109.8 4.9 %collective-permute-done.4 = bf16[2,216,256]{2,1,0:T(8,128)(2,1)S(1)} collective-permute-done((bf16[2,216,256]{2,1,0:T(8,128)(2,1)S(1)}, bf16[2,216,256]{2,1,0:T(8,128)(2,1)S(1)}, u32[]{:S(2)}, u32[]{:S(2)}) %collective-permute-start.4) | collective-permute-done | bytes 221216 | tf_op jit(solution)/shard_map/ppermute | solution.py:14
  116.4 4.6 %collective-permute-start.5 = (bf16[2,216,256]{2,1,0:T(8,128)(2,1)S(1)}, bf16[2,216,256]{2,1,0:T(8,128)(2,1)S(1)}, u32[]{:S(2)}, u32[]{:S(2)}) collective-permute-start(bf16[2,216,256]{2,1,0:T(8,128)(2,1)S(1)} %fusion.112), channel_id=1, source_target_pairs={{0,32},{32,0},{8,40},{40,8},{16,48},{48,16},{24,56},{56,24},{1,33}... | collective-permute-start | bytes 663560 | tf_op jit(solution)/shard_map/ppermute | solution.py:14
  121.5 4.1 %collective-permute-done.5 = bf16[2,216,256]{2,1,0:T(8,128)(2,1)S(1)} collective-permute-done((bf16[2,216,256]{2,1,0:T(8,128)(2,1)S(1)}, bf16[2,216,256]{2,1,0:T(8,128)(2,1)S(1)}, u32[]{:S(2)}, u32[]{:S(2)}) %collective-permute-start.5) | collective-permute-done | bytes 221216 | tf_op jit(solution)/shard_map/ppermute | solution.py:14
  127.1 2.6 %collective-permute-start.6 = (bf16[2,216,256]{2,1,0:T(8,128)(2,1)S(1)}, bf16[2,216,256]{2,1,0:T(8,128)(2,1)S(1)}, u32[]{:S(2)}, u32[]{:S(2)}) collective-permute-start(bf16[2,216,256]{2,1,0:T(8,128)(2,1)S(1)} %fusion.110), channel_id=1, source_target_pairs={{0,1},{1,0},{2,3},{3,2},{4,5},{5,4},{6,7},{7,6},{8,9},{9,8},{10,11... | collective-permute-start | bytes 663560 | tf_op jit(solution)/shard_map/ppermute | solution.py:14
  130.2 3.6 %collective-permute-done.6 = bf16[2,216,256]{2,1,0:T(8,128)(2,1)S(1)} collective-permute-done((bf16[2,216,256]{2,1,0:T(8,128)(2,1)S(1)}, bf16[2,216,256]{2,1,0:T(8,128)(2,1)S(1)}, u32[]{:S(2)}, u32[]{:S(2)}) %collective-permute-start.6) | collective-permute-done | bytes 221216 | tf_op jit(solution)/shard_map/ppermute | solution.py:14
  134.4 3.1 %collective-permute-start.7 = (bf16[2,216,256]{2,1,0:T(8,128)(2,1)S(1)}, bf16[2,216,256]{2,1,0:T(8,128)(2,1)S(1)}, u32[]{:S(2)}, u32[]{:S(2)}) collective-permute-start(bf16[2,216,256]{2,1,0:T(8,128)(2,1)S(1)} %fusion.108), channel_id=1, source_target_pairs={{0,2},{2,0},{1,3},{3,1},{4,6},{6,4},{5,7},{7,5},{8,10},{10,8},{9,1... | collective-permute-start | bytes 663560 | tf_op jit(solution)/shard_map/ppermute | solution.py:14
  138.0 10.1 %collective-permute-done.7 = bf16[2,216,256]{2,1,0:T(8,128)(2,1)S(1)} collective-permute-done((bf16[2,216,256]{2,1,0:T(8,128)(2,1)S(1)}, bf16[2,216,256]{2,1,0:T(8,128)(2,1)S(1)}, u32[]{:S(2)}, u32[]{:S(2)}) %collective-permute-start.7) | collective-permute-done | bytes 221216 | tf_op jit(solution)/shard_map/ppermute | solution.py:14
  148.8 4.0 %collective-permute-start.8 = (bf16[2,216,256]{2,1,0:T(8,128)(2,1)S(1)}, bf16[2,216,256]{2,1,0:T(8,128)(2,1)S(1)}, u32[]{:S(2)}, u32[]{:S(2)}) collective-permute-start(bf16[2,216,256]{2,1,0:T(8,128)(2,1)S(1)} %fusion.106), channel_id=1, source_target_pairs={{0,4},{4,0},{1,5},{5,1},{2,6},{6,2},{3,7},{7,3},{8,12},{12,8},{9,1... | collective-permute-start | bytes 663560 | tf_op jit(solution)/shard_map/ppermute | solution.py:14
  153.2 21.4 %collective-permute-done.8 = bf16[2,216,256]{2,1,0:T(8,128)(2,1)S(1)} collective-permute-done((bf16[2,216,256]{2,1,0:T(8,128)(2,1)S(1)}, bf16[2,216,256]{2,1,0:T(8,128)(2,1)S(1)}, u32[]{:S(2)}, u32[]{:S(2)}) %collective-permute-start.8) | collective-permute-done | bytes 221216 | tf_op jit(solution)/shard_map/ppermute | solution.py:14
  (167 shorter events, 59.0 us)
Async XLA Ops:
  0.0 58.1 %copy-start = (bf16[2,2,216,216]{3,2,1,0:T(8,128)(2,1)S(1)}, bf16[2,2,216,216]{3,2,1,0:T(8,128)(2,1)}, u32[]{:S(2)}) copy-start(bf16[2,2,216,216]{3,2,1,0:T(8,128)(2,1)} %param.7) | copy-start | bytes 1119748
  8.4 67.5 %collective-permute-start = (bf16[2,216,256]{2,1,0:T(8,128)(2,1)}, bf16[2,216,256]{2,1,0:T(8,128)(2,1)}, u32[]{:S(2)}, u32[]{:S(2)}) collective-permute-start(bf16[2,216,256]{2,1,0:T(8,128)(2,1)} %fusion.122), channel_id=1, source_target_pairs={{0,64},{64,0},{128,192},{192,128},{256,320},{320,256},{384,448},{4... | collective-permute-start | bytes 663560 | tf_op jit(solution)/shard_map/ppermute | solution.py:14
  63.1 1.0 copy-start.2
  64.2 1.0 copy-start.1
  65.2 1.0 copy-start.4
  66.2 1.0 copy-start.3
  67.3 1.0 copy-start.6
  68.3 1.0 copy-start.5
  75.8 2.0 %copy-start.13 = (f32[2,256,216]{1,2,0:T(8,128)S(1)}, f32[2,256,216]{1,2,0:T(8,128)}, u32[]{:S(2)}) copy-start(f32[2,256,216]{1,2,0:T(8,128)} %fusion.149) | copy-start | bytes 1327108
  77.8 1.3 copy-start.25
  77.8 1.3 copy-start.26
  79.3 7.9 %collective-permute-start.1 = (bf16[2,216,256]{2,1,0:T(8,128)(2,1)S(1)}, bf16[2,216,256]{2,1,0:T(8,128)(2,1)S(1)}, u32[]{:S(2)}, u32[]{:S(2)}) collective-permute-start(bf16[2,216,256]{2,1,0:T(8,128)(2,1)S(1)} %fusion.120), channel_id=1, source_target_pairs={{0,128},{128,0},{64,192},{192,64},{256,384},{384,256},{320,448},{4... | collective-permute-start | bytes 663560 | tf_op jit(solution)/shard_map/ppermute | solution.py:14
  87.5 1.1 copy-start.24
  88.8 8.6 %collective-permute-start.2 = (bf16[2,216,256]{2,1,0:T(8,128)(2,1)S(1)}, bf16[2,216,256]{2,1,0:T(8,128)(2,1)S(1)}, u32[]{:S(2)}, u32[]{:S(2)}) collective-permute-start(bf16[2,216,256]{2,1,0:T(8,128)(2,1)S(1)} %fusion.118), channel_id=1, source_target_pairs={{0,256},{256,0},{64,320},{320,64},{128,384},{384,128},{192,448},{4... | collective-permute-start | bytes 663560 | tf_op jit(solution)/shard_map/ppermute | solution.py:14
  97.6 1.1 copy-start.22
  99.0 5.7 %collective-permute-start.3 = (bf16[2,216,256]{2,1,0:T(8,128)(2,1)S(1)}, bf16[2,216,256]{2,1,0:T(8,128)(2,1)S(1)}, u32[]{:S(2)}, u32[]{:S(2)}) collective-permute-start(bf16[2,216,256]{2,1,0:T(8,128)(2,1)S(1)} %fusion.116), channel_id=1, source_target_pairs={{0,8},{8,0},{16,24},{24,16},{32,40},{40,32},{48,56},{56,48},{1,9},... | collective-permute-start | bytes 663560 | tf_op jit(solution)/shard_map/ppermute | solution.py:14
  104.9 1.1 copy-start.20
  106.3 8.5 %collective-permute-start.4 = (bf16[2,216,256]{2,1,0:T(8,128)(2,1)S(1)}, bf16[2,216,256]{2,1,0:T(8,128)(2,1)S(1)}, u32[]{:S(2)}, u32[]{:S(2)}) collective-permute-start(bf16[2,216,256]{2,1,0:T(8,128)(2,1)S(1)} %fusion.114), channel_id=1, source_target_pairs={{0,16},{16,0},{8,24},{24,8},{32,48},{48,32},{40,56},{56,40},{1,17}... | collective-permute-start | bytes 663560 | tf_op jit(solution)/shard_map/ppermute | solution.py:14
  115.0 1.1 copy-start.18
  116.4 9.2 %collective-permute-start.5 = (bf16[2,216,256]{2,1,0:T(8,128)(2,1)S(1)}, bf16[2,216,256]{2,1,0:T(8,128)(2,1)S(1)}, u32[]{:S(2)}, u32[]{:S(2)}) collective-permute-start(bf16[2,216,256]{2,1,0:T(8,128)(2,1)S(1)} %fusion.112), channel_id=1, source_target_pairs={{0,32},{32,0},{8,40},{40,8},{16,48},{48,16},{24,56},{56,24},{1,33}... | collective-permute-start | bytes 663560 | tf_op jit(solution)/shard_map/ppermute | solution.py:14
  125.7 1.1 copy-start.16
  127.1 6.7 %collective-permute-start.6 = (bf16[2,216,256]{2,1,0:T(8,128)(2,1)S(1)}, bf16[2,216,256]{2,1,0:T(8,128)(2,1)S(1)}, u32[]{:S(2)}, u32[]{:S(2)}) collective-permute-start(bf16[2,216,256]{2,1,0:T(8,128)(2,1)S(1)} %fusion.110), channel_id=1, source_target_pairs={{0,1},{1,0},{2,3},{3,2},{4,5},{5,4},{6,7},{7,6},{8,9},{9,8},{10,11... | collective-permute-start | bytes 663560 | tf_op jit(solution)/shard_map/ppermute | solution.py:14
  134.4 13.6 %collective-permute-start.7 = (bf16[2,216,256]{2,1,0:T(8,128)(2,1)S(1)}, bf16[2,216,256]{2,1,0:T(8,128)(2,1)S(1)}, u32[]{:S(2)}, u32[]{:S(2)}) collective-permute-start(bf16[2,216,256]{2,1,0:T(8,128)(2,1)S(1)} %fusion.108), channel_id=1, source_target_pairs={{0,2},{2,0},{1,3},{3,1},{4,6},{6,4},{5,7},{7,5},{8,10},{10,8},{9,1... | collective-permute-start | bytes 663560 | tf_op jit(solution)/shard_map/ppermute | solution.py:14
  148.8 25.9 %collective-permute-start.8 = (bf16[2,216,256]{2,1,0:T(8,128)(2,1)S(1)}, bf16[2,216,256]{2,1,0:T(8,128)(2,1)S(1)}, u32[]{:S(2)}, u32[]{:S(2)}) collective-permute-start(bf16[2,216,256]{2,1,0:T(8,128)(2,1)S(1)} %fusion.106), channel_id=1, source_target_pairs={{0,4},{4,0},{1,5},{5,1},{2,6},{6,2},{3,7},{7,3},{8,12},{12,8},{9,1... | collective-permute-start | bytes 663560 | tf_op jit(solution)/shard_map/ppermute | solution.py:14
  (13 other events, 13.3 us)
where the time goes:
time: 177 us; the launch traced here: 176 us
  local copies, waits for them, and re-layouts  61.4 us (35%)
  waiting for transfers between devices  52.1 us (29%)
  starting transfers between devices  46.7 us (26%)
  matrix products  11.3 us (6%)
  other arithmetic  3.51 us (2%)
    ppermute x9, waiting for transfers between devices, swapped(): return lax.ppermute(block, axis, route)  52.1 us
    ppermute x9, starting transfers between devices, swapped(): return lax.ppermute(block, axis, route)  46.7 us
    gather x18, local copies, waits for them, and re-layouts, rotate(): sines = jnp.take(sin_tab, labels, axis=1)  24.5 us
    gather x18, local copies, waits for them, and re-layouts, rotate(): cosines = jnp.take(cos_tab, labels, axis=1)  24.5 us
    unnamed x57, local copies, waits for them, and re-layouts  10.5 us
    dot_general x18, matrix products, combine(): jnp.einsum('jk,rkh->rjh', far_mats[target], received, preferred_element_t...  5.81 us
    dot_general x18, matrix products, combine(): jnp.einsum('jk,rkh->rjh', own_mats[target], kept_half, preferred_element_...  5.53 us
  transfers between devices with their start and end apart: 9, of which 8 were waited for; matrix products, arithmetic and copies ran while one was open for 29% of the time, Pallas kernels for 0%

commit v1 on v0

v1 whole, which is shorter than its diff:
```python
import functools

import jax
import jax.numpy as jnp
from jax import lax
from jax.experimental import pallas as pl
from jax.experimental.pallas import tpu as pltpu
from jax.sharding import Mesh, PartitionSpec as P

K = 216
KP = 256
HALF = 256
ROWS = 256
LEVELS = 9
AXES = ("y", "zh", "x", "core", "zl")
BACK = ("y", "x", "core", "zl")
ID_LANE = K
HIGH_BITS = (6, 7, 3, 4, 5)
LOW_BITS = (5, 6, 7)
f32 = jnp.float32
bf16 = jnp.bfloat16


def dot(a, b):
    return jnp.dot(a, b, preferred_element_type=f32)


def turn(ids, state, tables):
    rows = ids.shape[0]
    boxes = lax.broadcasted_iota(jnp.int32, (rows, KP), 1).astype(f32)
    picked = dot(jnp.where(ids == boxes, 1.0, 0.0).astype(bf16), tables)
    cosines, sines = picked[:, :KP], picked[:, KP:]
    re, im = state[:, :KP], state[:, KP:]
    return cosines * re - sines * im, sines * re + cosines * im


def split(plane, block):
    parts = plane.reshape(plane.shape[0] // (2 * block), 2, block, KP)
    half = plane.shape[0] // 2
    return jnp.concatenate(
        [parts[:, 0].reshape(half, KP), parts[:, 1].reshape(half, KP)], axis=1
    ).astype(bf16)


def level(state, ids, tables, mats, bit):
    block = 1 << bit
    stacked = []
    for half in range(2):
        re, im = turn(ids[half], state[half], tables)
        stacked += [split(re, block), split(im, block)]
    mixed = dot(jnp.concatenate(stacked, axis=0), mats)
    quarter = ROWS // 2
    fresh = []
    for target in range(2):
        planes = []
        for plane in range(2):
            pieces = [
                mixed[
                    (2 * half + plane) * quarter : (2 * half + plane + 1) * quarter,
                    target * KP : (target + 1) * KP,
                ].reshape(quarter // block, 1, block, KP)
                for half in range(2)
            ]
            planes.append(jnp.concatenate(pieces, axis=1).reshape(ROWS, KP))
        fresh.append(jnp.concatenate(planes, axis=1).astype(bf16).astype(f32))
    return fresh


def butterfly(side_ref, got_ref, tab_ref, mat_ref, order_ref, out_ref):
    tables = tab_ref[...]
    mats = mat_ref[...]
    got = got_ref[...].astype(f32)
    re, im = turn(got[:, ID_LANE : ID_LANE + 1], got, tables)
    mixed = dot(jnp.concatenate([split(re, 64), split(im, 64)], axis=0), mats)
    state = [
        jnp.concatenate(
            [
                mixed[:ROWS, target * KP : (target + 1) * KP],
                mixed[ROWS:, target * KP : (target + 1) * KP],
            ],
            axis=1,
        ).astype(bf16).astype(f32)
        for target in range(2)
    ]
    labels = got[:, 128:256].reshape(4, 2, 64, 128)
    labels = jnp.where(side_ref[0] == 0, labels[:, 0], labels[:, 1]).reshape(ROWS, 128)
    first = ID_LANE - 128 + 1

    def ids(table, number):
        return [
            table[:, first + 8 * half + number - 1 : first + 8 * half + number]
            for half in range(2)
        ]

    for number, bit in enumerate(HIGH_BITS, 1):
        state = level(state, ids(labels, number), tables, mats, bit)
    order = order_ref[...]
    labels = dot(order[:ROWS], labels.astype(bf16))
    state = [dot(order[:ROWS], half.astype(bf16)) for half in state]
    for number, bit in enumerate(LOW_BITS, 6):
        state = level(state, ids(labels, number), tables, mats, bit)
    for half in range(2):
        out_ref[:, half * 512 : (half + 1) * 512] = dot(
            order[ROWS:], state[half].astype(bf16)
        ).astype(bf16)


def apply_levels(side, got, tables, mats, order):
    vmem = pl.BlockSpec(memory_space=pltpu.VMEM)
    return pl.pallas_call(
        butterfly,
        out_shape=jax.ShapeDtypeStruct((ROWS, 1024), bf16),
        in_specs=[pl.BlockSpec(memory_space=pltpu.SMEM)] + [vmem] * 4,
        out_specs=vmem,
        name="butterfly",
    )(side, got, tables, mats, order)


def row_order():
    row = jnp.arange(ROWS)
    moved = (row & 31) * 8 + (row >> 5)
    there = (moved[:, None] == row[None, :]).astype(bf16)
    return jnp.concatenate([there, there.T], axis=0)


def pack_tables(angles):
    wide = jnp.pad(jnp.stack([jnp.cos(angles), jnp.sin(angles)]), ((0, 0), (0, KP - K), (0, 0)))
    return wide.transpose(2, 0, 1).reshape(256, 2 * KP).astype(bf16)


def pack_mats(translate):
    wide = jnp.pad(translate, ((0, 0), (0, 0), (0, KP - K), (0, KP - K)))
    return wide.transpose(1, 3, 0, 2).reshape(2 * KP, 2 * KP)


def pack_columns(weights, box_ids):
    cols = weights.shape[2]
    il = cols // 2
    later = box_ids[1:]
    rows = jnp.concatenate(
        [
            box_ids[:1],
            jnp.tile(later[:, :il], (1, 2)),
            jnp.tile(later[:, il:], (1, 2)),
        ],
        axis=0,
    ).astype(bf16)
    first = jnp.concatenate([weights[0], rows, jnp.zeros((KP - K - 17, cols), bf16)], axis=0)
    second = jnp.pad(weights[1], ((0, KP - K), (0, 0)))
    return jnp.concatenate([first, second], axis=0).T


def shards(weights, translate, angles, box_ids):
    packed = pack_columns(weights, box_ids)
    packed = packed.reshape(2, 4, 64, 512).transpose(1, 0, 2, 3).reshape(512, 4, 128)
    got = lax.all_to_all(packed, AXES, 0, 0, tiled=True).reshape(512, 512)
    side = lax.axis_index("zh").reshape(1)
    out = apply_levels(side, got, pack_tables(angles), pack_mats(translate), row_order())
    back = lax.all_to_all(out.reshape(256, 8, 128), BACK, 0, 0, tiled=True)
    back = back.reshape(256, 2, 2, KP)[:, :, :, :K]
    return back.transpose(2, 3, 1, 0).reshape(2, K, 512)


def solution(mesh):
    grid = Mesh(mesh.devices.reshape(4, 2, 4, 2, 8), AXES)
    columns = P(None, None, AXES)
    return jax.shard_map(
        shards,
        mesh=grid,
        in_specs=(columns, P(), P(), P(None, AXES)),
        out_specs=columns,
        check_vma=False,
    )
```

time: 177 us -> 119 us (0.67)
  local copies, waits for them, and re-layouts: 61.4 us -> 10.6 us
  blocking collectives: 0 us -> 40.9 us
  starting transfers between devices: 46.7 us -> 24.3 us
  waiting for transfers between devices: 52.1 us -> 31.9 us
  matrix products: 11.3 us -> 0 us
  Pallas kernels: 0 us -> 7.2 us
    ppermute x9 -> x0, waiting for transfers between devices: 52.1 us -> none  [swapped(): return lax.ppermute(block, axis, route)]
    gather x36 -> x0, local copies, waits for them, and re-layouts: 48.9 us -> none  [the longest x18 24.5 us: rotate(): sines = jnp.take(sin_tab, labels, axis=1)]
    ppermute x9 -> x0, starting transfers between devices: 46.7 us -> none  [swapped(): return lax.ppermute(block, axis, route)]
    all_to_all x0 -> x1, blocking collectives: none -> 40.9 us  [shards(): back = lax.all_to_all(out.reshape(256, 8, 128), BACK, 0, 0, tiled=True)]
    all_to_all x0 -> x1, waiting for transfers between devices: none -> 31.9 us  [shards(): got = lax.all_to_all(packed, AXES, 0, 0, tiled=True).reshape(512, 512)]
    all_to_all x0 -> x1, starting transfers between devices: none -> 24.3 us  [shards(): got = lax.all_to_all(packed, AXES, 0, 0, tiled=True).reshape(512, 512)]
    dot_general x36 -> x0, matrix products: 11.3 us -> none  [the longest x18 5.81 us: combine(): jnp.einsum('jk,rkh->rjh', far_mats[target], received, preferred_element_t...]
    pallas_call x0 -> x1, Pallas kernels: none -> 7.2 us  [apply_levels(): pl.pallas_call(butterfly, out_shape=jax.ShapeDtypeStruct((ROWS, 1024), bf...]
  transfers between devices with their start and end apart: 9 -> 1, of which waited for: 8 -> 1; matrix products, arithmetic and copies ran while one was open for 29% -> 3% of each run, Pallas kernels for 0% -> 0%
where the time goes in v1:
time: 119 us; the launch traced here: 118 us
  blocking collectives  40.9 us (34%)
  waiting for transfers between devices  31.9 us (27%)
  starting transfers between devices  24.3 us (20%)
  local copies, waits for them, and re-layouts  10.6 us (9%)
  Pallas kernels  7.2 us (6%)
  other arithmetic  3.1 us (3%)
    all_to_all x1, blocking collectives, shards(): back = lax.all_to_all(out.reshape(256, 8, 128), BACK, 0, 0, tiled=True)  40.9 us
    all_to_all x1, waiting for transfers between devices, shards(): got = lax.all_to_all(packed, AXES, 0, 0, tiled=True).reshape(512, 512)  31.9 us
    all_to_all x1, starting transfers between devices, shards(): got = lax.all_to_all(packed, AXES, 0, 0, tiled=True).reshape(512, 512)  24.3 us
    pallas_call x1, Pallas kernels, apply_levels(): pl.pallas_call(butterfly, out_shape=jax.ShapeDtypeStruct((ROWS, 1024), bf...  7.2 us
    unnamed x11, local copies, waits for them, and re-layouts  5.02 us
  transfers between devices with their start and end apart: 1, of which 1 were waited for; matrix products, arithmetic and copies ran while one was open for 3% of the time, Pallas kernels for 0%

profile of v1, /device:TPU:1, one launch (start us, length us, event | category | flops | bytes accessed | tf_op | source)
XLA Modules:
  0.0 118.2 jit_solution(12469130028082673724)
XLA Ops:
  0.0 0.7 slice_convert_fusion.2
  0.7 0.7 slice_convert_fusion
  1.5 0.1 copy.20
  1.7 0.2 copy.28
  1.9 1.1 fusion.7
  3.0 0.1 copy.29
  3.1 0.1 copy.27
  3.4 0.4 concatenate.11
  3.9 0.9 reshape.44
  4.8 24.3 %all-to-all-start = ((bf16[512,4,128]{2,1,0:T(4,128)(2,1)}), bf16[512,4,128]{2,1,0:T(4,128)(2,1)S(1)}, u32[]{:S(2)}, u32[]{:S(2)}) async-start(bf16[512,4,128]{2,1,0:T(4,128)(2,1)} %reshape.44), calls=%async_computation | async-start | bytes 1048576 | tf_op jit(solution)/shard_map/all_to_all | solution.py:156
  29.1 0.8 fusion.3
  29.9 0.8 copy.26.tab_ref
  30.8 0.1 copy-done
  31.0 0.5 copy.24
  31.4 0.9 copy.32
  32.4 0.7 add_convert_fusion.order_ref
  33.2 31.9 %all-to-all-done = bf16[512,4,128]{2,1,0:T(4,128)(2,1)S(1)} async-done(((bf16[512,4,128]{2,1,0:T(4,128)(2,1)}), bf16[512,4,128]{2,1,0:T(4,128)(2,1)S(1)}, u32[]{:S(2)}, u32[]{:S(2)}) %all-to-all-start) | async-done | bytes 524320 | tf_op jit(solution)/shard_map/all_to_all | solution.py:156
  65.1 0.9 copy.35
  66.0 7.2 %butterfly.1 = bf16[256,1024]{1,0:T(8,128)(2,1)} custom-call(s32[1]{0:T(128)} %bitcast.side_ref, bf16[512,512]{1,0:T(8,128)(2,1)} %bitcast.34, bf16[256,512]{1,0:T(8,128)(2,1)} %copy.26.tab_ref, bf16[512,512]{1,0:T(8,128)(2,1)} %bitcast.32, bf16[512,256]{1,0:T(8,128)(2,1)} %add_convert_fusion.order_ref), custom_call_target="tpu_custom_call" | custom-call | tf_op jit(solution)/shard_map/butterfly/pallas_call | solution.py:110
  73.2 1.1 copy.33
  74.3 40.9 %all_to_all.10 = bf16[256,8,128]{2,1,0:T(8,128)(2,1)S(1)} all-to-all(bf16[256,8,128]{2,1,0:T(8,128)(2,1)S(1)} %bitcast.38), channel_id=1, replica_groups=mesh['y'=4,'zh'=2,'x'=4,'core'=2,'zl'=8] {'y','x','core','zl'}, dimensions={0} | all-to-all | bytes 1048576 | tf_op jit(solution)/shard_map/all_to_all | solution.py:159
  115.3 0.3 reshape.48
  115.6 1.6 %copy.30 = bf16[256,2,2,216]{0,1,3,2:T(2,128)(2,1)S(1)} copy(bf16[256,2,2,216]{3,2,1,0:T(2,128)(2,1)S(1)} %bitcast.39) | data formatting | bytes 884736
  117.2 1.0 reshape.49
  (13 shorter events, 0.5 us)
Async XLA Ops:
  4.8 24.3 %copy-start.1 = (f32[216,256]{1,0:T(8,128)S(1)}, f32[216,256]{1,0:T(8,128)}, u32[]{:S(2)}) copy-start(f32[216,256]{1,0:T(8,128)} %param.6) | copy-start | bytes 663556
  4.8 60.3 %all-to-all-start = ((bf16[512,4,128]{2,1,0:T(4,128)(2,1)}), bf16[512,4,128]{2,1,0:T(4,128)(2,1)S(1)}, u32[]{:S(2)}, u32[]{:S(2)}) async-start(bf16[512,4,128]{2,1,0:T(4,128)(2,1)} %reshape.44), calls=%async_computation | async-start | bytes 1048576 | tf_op jit(solution)/shard_map/all_to_all | solution.py:156
  29.9 1.0 copy-start

commit v2 on v1

--- a/solution.py
+++ b/solution.py
@@ -1,5 +1,3 @@
-import functools
-
 import jax
 import jax.numpy as jnp
 from jax import lax
@@ -14,7 +12,7 @@
 LEVELS = 9
 AXES = ("y", "zh", "x", "core", "zl")
 BACK = ("y", "x", "core", "zl")
-ID_LANE = K
+ID_LANE = K + 16
 HIGH_BITS = (6, 7, 3, 4, 5)
 LOW_BITS = (5, 6, 7)
 f32 = jnp.float32
@@ -66,10 +64,13 @@
     return fresh
 
 
-def butterfly(side_ref, got_ref, tab_ref, mat_ref, order_ref, out_ref):
+def butterfly(side_ref, got_ref, tab_ref, mat_ref, order_ref, out_ref, rows_ref):
     tables = tab_ref[...]
     mats = mat_ref[...]
-    got = got_ref[...].astype(f32)
+    rows_ref[...] = got_ref[...].astype(f32)
+    got = jnp.concatenate(
+        [rows_ref[pl.ds(part, 2 * ROWS, stride=4), :] for part in range(4)], axis=1
+    )
     re, im = turn(got[:, ID_LANE : ID_LANE + 1], got, tables)
     mixed = dot(jnp.concatenate([split(re, 64), split(im, 64)], axis=0), mats)
     state = [
@@ -84,7 +85,7 @@
     ]
     labels = got[:, 128:256].reshape(4, 2, 64, 128)
     labels = jnp.where(side_ref[0] == 0, labels[:, 0], labels[:, 1]).reshape(ROWS, 128)
-    first = ID_LANE - 128 + 1
+    first = K - 128
 
     def ids(table, number):
         return [
@@ -100,20 +101,96 @@
     for number, bit in enumerate(LOW_BITS, 6):
         state = level(state, ids(labels, number), tables, mats, bit)
     for half in range(2):
-        out_ref[:, half * 512 : (half + 1) * 512] = dot(
-            order[ROWS:], state[half].astype(bf16)
-        ).astype(bf16)
+        done = dot(order[ROWS:], state[half].astype(bf16))
+        for part in range(4):
+            rows_ref[pl.ds(4 * half + part, ROWS, stride=8), :] = done[
+                :, part * 128 : (part + 1) * 128
+            ]
+    out_ref[...] = rows_ref[...].astype(bf16)
+
+
+VMEM = pl.BlockSpec(memory_space=pltpu.VMEM)
 
 
 def apply_levels(side, got, tables, mats, order):
-    vmem = pl.BlockSpec(memory_space=pltpu.VMEM)
     return pl.pallas_call(
         butterfly,
-        out_shape=jax.ShapeDtypeStruct((ROWS, 1024), bf16),
-        in_specs=[pl.BlockSpec(memory_space=pltpu.SMEM)] + [vmem] * 4,
-        out_specs=vmem,
+        out_shape=jax.ShapeDtypeStruct((2048, 128), bf16),
+        in_specs=[pl.BlockSpec(memory_space=pltpu.SMEM)] + [VMEM] * 4,
+        out_specs=VMEM,
+        scratch_shapes=[pltpu.VMEM((2048, 128), f32)],
+        compiler_params=pltpu.CompilerParams(vmem_limit_bytes=24 * 2**20),
         name="butterfly",
     )(side, got, tables, mats, order)
+
+
+def across(a, b):
+    return lax.dot_general(a, b, (((1,), (1,)), ((), ())), preferred_element_type=f32)
+
+
+def pack(weights_ref, ids_ref, out_ref, rows_ref):
+    cols = 2 * ROWS
+    ids = ids_ref[...].astype(f32)
+    low, high = ids[1:, :ROWS], ids[1:, ROWS:]
+    labels = jnp.concatenate(
+        [
+            jnp.concatenate([low, low], axis=1),
+            jnp.concatenate([high, high], axis=1),
+            jnp.broadcast_to(ids[:1], (KP - K - 16, cols)),
+        ],
+        axis=0,
+    )
+    target = lax.broadcasted_iota(jnp.int32, (cols, cols), 0)
+    source = lax.broadcasted_iota(jnp.int32, (cols, cols), 1)
+    wanted = (target & 64) * 4 + (target >> 7) * 64 + (target & 63)
+    chosen = jnp.where(source == wanted, 1.0, 0.0).astype(bf16)
+    first = jnp.concatenate([weights_ref[0].astype(f32), labels], axis=0).astype(bf16)
+    planes = [across(chosen, first), across(chosen, weights_ref[1])]
+    rows_ref[pl.ds(0, cols, stride=4), :] = planes[0][:, :128]
+    rows_ref[pl.ds(1, cols, stride=4), :] = planes[0][:, 128:]
+    rows_ref[pl.ds(2, cols, stride=4), :] = planes[1][:, :128]
+    rows_ref[pl.ds(3, cols, stride=4), :] = jnp.concatenate(
+        [planes[1][:, 128:], jnp.zeros((cols, KP - K), f32)], axis=1
+    )
+    out_ref[...] = rows_ref[...].astype(bf16)
+
+
+def pack_columns(weights, box_ids):
+    return pl.pallas_call(
+        pack,
+        out_shape=jax.ShapeDtypeStruct((2048, 128), bf16),
+        in_specs=[VMEM] * 2,
+        out_specs=VMEM,
+        scratch_shapes=[pltpu.VMEM((2048, 128), f32)],
+        name="pack",
+    )(weights, box_ids)
+
+
+def unpack(back_ref, out_ref, rows_ref):
+    rows_ref[...] = back_ref[...].astype(f32)
+    here = lax.broadcasted_iota(jnp.int32, (128, 128), 0)
+    there = lax.broadcasted_iota(jnp.int32, (128, 128), 1)
+    same = jnp.where(here == there, 1.0, 0.0).astype(bf16)
+    for plane in range(2):
+        for half in range(2):
+            pieces = [
+                across(same, rows_ref[pl.ds(4 * half + 2 * plane + part, ROWS, stride=8), :].astype(bf16))
+                for part in range(2)
+            ]
+            block = jnp.concatenate([pieces[0], pieces[1][: K - 128]], axis=0)
+            out_ref[plane, :, half * ROWS : (half + 1) * ROWS] = block.astype(bf16)
+
+
+def unpack_columns(back):
+    return pl.pallas_call(
+        unpack,
+        out_shape=jax.ShapeDtypeStruct((2, K, 512), bf16),
+        in_specs=[VMEM],
+        out_specs=VMEM,
+        scratch_shapes=[pltpu.VMEM((2048, 128), f32)],
+        compiler_params=pltpu.CompilerParams(vmem_limit_bytes=12 * 2**20),
+        name="unpack",
+    )(back)
 
 
 def row_order():
@@ -133,32 +210,13 @@
     return wide.transpose(1, 3, 0, 2).reshape(2 * KP, 2 * KP)
 
 
-def pack_columns(weights, box_ids):
-    cols = weights.shape[2]
-    il = cols // 2
-    later = box_ids[1:]
-    rows = jnp.concatenate(
-        [
-            box_ids[:1],
-            jnp.tile(later[:, :il], (1, 2)),
-            jnp.tile(later[:, il:], (1, 2)),
-        ],
-        axis=0,
-    ).astype(bf16)
-    first = jnp.concatenate([weights[0], rows, jnp.zeros((KP - K - 17, cols), bf16)], axis=0)
-    second = jnp.pad(weights[1], ((0, KP - K), (0, 0)))
-    return jnp.concatenate([first, second], axis=0).T
-
-
 def shards(weights, translate, angles, box_ids):
-    packed = pack_columns(weights, box_ids)
-    packed = packed.reshape(2, 4, 64, 512).transpose(1, 0, 2, 3).reshape(512, 4, 128)
-    got = lax.all_to_all(packed, AXES, 0, 0, tiled=True).reshape(512, 512)
+    packed = pack_columns(weights, box_ids).reshape(512, 4, 128)
+    got = lax.all_to_all(packed, AXES, 0, 0, tiled=True).reshape(2048, 128)
     side = lax.axis_index("zh").reshape(1)
     out = apply_levels(side, got, pack_tables(angles), pack_mats(translate), row_order())
     back = lax.all_to_all(out.reshape(256, 8, 128), BACK, 0, 0, tiled=True)
-    back = back.reshape(256, 2, 2, KP)[:, :, :, :K]
-    return back.transpose(2, 3, 1, 0).reshape(2, K, 512)
+    return unpack_columns(back.reshape(2048, 128))
 
 
 def solution(mesh):

time: 119 us -> 110 us (0.924)
  local copies, waits for them, and re-layouts: 10.6 us -> 1.59 us
  other arithmetic: 3.1 us -> 0.96 us
  waiting for transfers between devices: 31.9 us -> 33.4 us
  Pallas kernels: 7.2 us -> 8.66 us
    unnamed x11 -> x5, local copies, waits for them, and re-layouts: 5.02 us -> 0.92 us
    reshape x3 -> x0, local copies, waits for them, and re-layouts: 2.29 us -> none  [the longest x1 1.04 us: shards(): return back.transpose(2, 3, 1, 0).reshape(2, K, 512)]
    all_to_all x1, waiting for transfers between devices: 31.9 us -> 33.4 us  [shards(): got = lax.all_to_all(packed, AXES, 0, 0, tiled=True).reshape(2048, 128)]
    another operation x2 -> x0, other arithmetic: 1.46 us -> none
    pallas_call x1 -> x3, Pallas kernels: 7.2 us -> 8.66 us  [the longest x1 5.18 us: apply_levels(): pl.pallas_call(butterfly, out_shape=jax.ShapeDtypeStruct((2048, 128), bf1...]
  transfers between devices with their start and end apart: 1 -> 1, of which waited for: 1 -> 1; matrix products, arithmetic and copies ran while one was open for 3% -> 2% of each run, Pallas kernels for 0% -> 0%
where the time goes in v2:
time: 110 us
  blocking collectives  40.7 us (37%)
  waiting for transfers between devices  33.4 us (30%)
  starting transfers between devices  24.3 us (22%)
  Pallas kernels  8.66 us (8%)
  local copies, waits for them, and re-layouts  1.59 us (1%)
    all_to_all x1, blocking collectives, shards(): back = lax.all_to_all(out.reshape(256, 8, 128), BACK, 0, 0, tiled=True)  40.7 us
    all_to_all x1, waiting for transfers between devices, shards(): got = lax.all_to_all(packed, AXES, 0, 0, tiled=True).reshape(2048, 128)  33.4 us
    all_to_all x1, starting transfers between devices, shards(): got = lax.all_to_all(packed, AXES, 0, 0, tiled=True).reshape(2048, 128)  24.3 us
    pallas_call x1, Pallas kernels, apply_levels(): pl.pallas_call(butterfly, out_shape=jax.ShapeDtypeStruct((2048, 128), bf1...  5.18 us
    pallas_call x1, Pallas kernels, pack_columns(): pl.pallas_call(pack, out_shape=jax.ShapeDtypeStruct((2048, 128), bf16), i...  2.34 us
  transfers between devices with their start and end apart: 1, of which 1 were waited for; matrix products, arithmetic and copies ran while one was open for 2% of the time, Pallas kernels for 0%

profile of v2, /device:TPU:1, one launch (start us, length us, event | category | flops | bytes accessed | tf_op | source)
XLA Modules:
  0.0 109.7 jit_solution(2640830289427312065)
XLA Ops:
  0.0 2.3 %pack.1 = bf16[2048,128]{1,0:T(8,128)(2,1)} custom-call(bf16[2,216,512]{2,1,0:T(8,128)(2,1)} %weights_ref.1, s32[9,512]{1,0:T(8,128)} %ids_ref.1), custom_call_target="tpu_custom_call" | custom-call | tf_op jit(solution)/shard_map/pack/pallas_call | solution.py:159
  2.3 0.0 copy-start.1
  2.3 24.3 %all-to-all-start = ((bf16[512,4,128]{2,1,0:T(4,128)(2,1)}), bf16[512,4,128]{2,1,0:T(4,128)(2,1)S(1)}, u32[]{:S(2)}, u32[]{:S(2)}) async-start(bf16[512,4,128]{2,1,0:T(4,128)(2,1)} %bitcast.21), calls=%async_computation | async-start | bytes 1048576 | tf_op jit(solution)/shard_map/all_to_all | solution.py:215
  26.6 0.0 copy-done.1
  26.7 0.8 fusion.3
  27.5 0.0 copy-start
  27.5 0.1 copy.7.tab_ref
  27.6 0.8 copy-done
  28.5 0.1 pad_bitcast_fusion
  28.5 0.5 copy.6
  29.0 0.1 copy.8
  29.1 0.1 iota_compare_fusion.2
  29.3 33.4 %all-to-all-done = bf16[512,4,128]{2,1,0:T(4,128)(2,1)S(1)} async-done(((bf16[512,4,128]{2,1,0:T(4,128)(2,1)}), bf16[512,4,128]{2,1,0:T(4,128)(2,1)S(1)}, u32[]{:S(2)}, u32[]{:S(2)}) %all-to-all-start) | async-done | bytes 524320 | tf_op jit(solution)/shard_map/all_to_all | solution.py:215
  62.7 5.2 %butterfly.1 = bf16[2048,128]{1,0:T(8,128)(2,1)S(1)} custom-call(s32[1]{0:T(128)} %bitcast.side_ref, bf16[2048,128]{1,0:T(8,128)(2,1)S(1)} %bitcast.17, bf16[256,512]{1,0:T(8,128)(2,1)S(1)} %copy.7.tab_ref, bf16[512,512]{1,0:T(8,128)(2,1)S(1)} %bitcast.18, bf16[512,256]{1,0:T(8,128)(2,1)S(1)} %add_convert_fusion.order_ref), custom_call_target="tpu_custom_call" | custom-call | tf_op jit(solution)/shard_map/butterfly/pallas_call | solution.py:116
  67.8 40.7 %all_to_all.10 = bf16[256,8,128]{2,1,0:T(8,128)(2,1)S(1)} all-to-all(bf16[256,8,128]{2,1,0:T(8,128)(2,1)S(1)} %bitcast.19), channel_id=1, replica_groups=mesh['y'=4,'zh'=2,'x'=4,'core'=2,'zl'=8] {'y','x','core','zl'}, dimensions={0} | all-to-all | bytes 1048576 | tf_op jit(solution)/shard_map/all_to_all | solution.py:218
  108.6 1.1 %unpack.1 = bf16[2,216,512]{2,1,0:T(8,128)(2,1)} custom-call(bf16[2048,128]{1,0:T(8,128)(2,1)S(1)} %bitcast.20), custom_call_target="tpu_custom_call" | custom-call | tf_op jit(solution)/shard_map/unpack/pallas_call | solution.py:185
  (3 shorter events, 0.1 us)
Async XLA Ops:
  2.3 24.3 %copy-start.1 = (f32[216,256]{1,0:T(8,128)S(1)}, f32[216,256]{1,0:T(8,128)}, u32[]{:S(2)}) copy-start(f32[216,256]{1,0:T(8,128)} %param.6) | copy-start | bytes 663556
  2.3 60.3 %all-to-all-start = ((bf16[512,4,128]{2,1,0:T(4,128)(2,1)}), bf16[512,4,128]{2,1,0:T(4,128)(2,1)S(1)}, u32[]{:S(2)}, u32[]{:S(2)}) async-start(bf16[512,4,128]{2,1,0:T(4,128)(2,1)} %bitcast.21), calls=%async_computation | async-start | bytes 1048576 | tf_op jit(solution)/shard_map/all_to_all | solution.py:215
  27.5 1.0 copy-start

commit v3 on v2

v3 whole, which is shorter than its diff:
```python
import jax
import jax.numpy as jnp
from jax import lax
from jax.experimental import pallas as pl
from jax.experimental.pallas import tpu as pltpu
from jax.sharding import Mesh, PartitionSpec as P

K = 216
KP = 256
HALF = 256
ROWS = 256
LEVELS = 9
AXES = ("y", "zh", "x", "core", "zl")
OUT = ("y", "zh", "x", "zl")
BACK = ("y", "x", "zl")
ID_LANE = K + 16
TAIL = K - 128
ROOM = 128 - TAIL
BITS = {1: 5, 2: 6, 4: 3, 5: 4, 6: 5, 7: 6, 8: 7}
f32 = jnp.float32
bf16 = jnp.bfloat16


def dot(a, b):
    return jnp.dot(a, b, preferred_element_type=f32)


def turn(ids, state, tables):
    rows = ids.shape[0]
    boxes = lax.broadcasted_iota(jnp.int32, (rows, KP), 1).astype(f32)
    picked = dot(jnp.where(ids == boxes, 1.0, 0.0).astype(bf16), tables)
    cosines, sines = picked[:, :KP], picked[:, KP:]
    re, im = state[:, :KP], state[:, KP:]
    return cosines * re - sines * im, sines * re + cosines * im


def split(plane, block):
    parts = plane.reshape(plane.shape[0] // (2 * block), 2, block, KP)
    half = plane.shape[0] // 2
    return jnp.concatenate(
        [parts[:, 0].reshape(half, KP), parts[:, 1].reshape(half, KP)], axis=1
    ).astype(bf16)


def level(state, ids, tables, mats, bit):
    block = 1 << bit
    stacked = []
    for half in range(2):
        re, im = turn(ids[half], state[half], tables)
        stacked += [split(re, block), split(im, block)]
    mixed = dot(jnp.concatenate(stacked, axis=0), mats)
    quarter = ROWS // 2
    fresh = []
    for target in range(2):
        planes = []
        for plane in range(2):
            pieces = [
                mixed[
                    (2 * half + plane) * quarter : (2 * half + plane + 1) * quarter,
                    target * KP : (target + 1) * KP,
                ].reshape(quarter // block, 1, block, KP)
                for half in range(2)
            ]
            planes.append(jnp.concatenate(pieces, axis=1).reshape(ROWS, KP))
        fresh.append(jnp.concatenate(planes, axis=1).astype(bf16).astype(f32))
    return fresh


def ids(labels, number):
    first = TAIL + number - 1
    return [labels[:, first + 8 * half : first + 8 * half + 1] for half in range(2)]


def round_to(values):
    return values.astype(bf16).astype(f32)


def opening(side_ref, got_ref, tab_ref, mat_ref, keep_ref, send_ref, label_ref, rows_ref):
    tables = tab_ref[...]
    mats = mat_ref[...]
    quarter = ROWS // 2
    rows_ref[...] = got_ref[...].astype(f32)
    stacked, labels = [], []
    for kept in range(2):
        got = jnp.concatenate(
            [rows_ref[pl.ds(4 * kept + part, ROWS, stride=8), :] for part in range(4)], axis=1
        )
        re, im = turn(got[:, ID_LANE : ID_LANE + 1], got, tables)
        stacked += [split(re, 32), split(im, 32)]
        tags = got[:, 128:256].reshape(4, 2, 32, 128)
        labels.append(jnp.where(side_ref[0] == 0, tags[:, 0], tags[:, 1]).reshape(quarter, 128))
    labels = jnp.concatenate(labels, axis=0)
    mixed = dot(jnp.concatenate(stacked, axis=0), mats)
    state = []
    for target in range(2):
        lanes = slice(target * KP, (target + 1) * KP)
        blocks = [mixed[n * quarter : (n + 1) * quarter, lanes] for n in range(4)]
        state.append(
            round_to(
                jnp.concatenate(
                    [
                        jnp.concatenate(blocks[:2], axis=1),
                        jnp.concatenate(blocks[2:], axis=1),
                    ],
                    axis=0,
                )
            )
        )
    for number in (1, 2):
        state = level(state, ids(labels, number), tables, mats, BITS[number])
    turned = [
        jnp.concatenate(turn(ids(labels, 3)[half], state[half], tables), axis=1).astype(bf16)
        for half in range(2)
    ]
    low = side_ref[1] == 0
    keep_ref[...] = jnp.where(low, turned[0], turned[1])
    send_ref[...] = jnp.where(low, turned[1], turned[0])
    label_ref[...] = labels.astype(bf16)


def tail_lanes(part):
    lane = lax.broadcasted_iota(jnp.int32, (ROWS // 2, 128), 1)
    return (lane >= part * ROOM) & (lane < (part + 1) * ROOM)


def closing(side_ref, keep_ref, got_ref, label_ref, tab_ref, mat_ref, order_ref, out_ref, rows_ref):
    tables = tab_ref[...]
    mats = mat_ref[...]
    labels = label_ref[...].astype(f32)
    flipped = jnp.concatenate([mats[KP:], mats[:KP]], axis=0)
    mixed = dot(
        jnp.concatenate(
            [
                jnp.concatenate([keep_ref[:, :KP], got_ref[:, :KP]], axis=1),
                jnp.concatenate([keep_ref[:, KP:], got_ref[:, KP:]], axis=1),
            ],
            axis=0,
        ),
        jnp.where(side_ref[1] == 0, mats, flipped),
    )
    state = [
        round_to(
            jnp.concatenate(
                [
                    mixed[:ROWS, target * KP : (target + 1) * KP],
                    mixed[ROWS:, target * KP : (target + 1) * KP],
                ],
                axis=1,
            )
        )
        for target in range(2)
    ]
    for number in (4, 5):
        state = level(state, ids(labels, number), tables, mats, BITS[number])
    order = order_ref[...]
    labels = dot(order[:ROWS], labels.astype(bf16))
    state = [dot(order[:ROWS], half.astype(bf16)) for half in state]
    for number in (6, 7, 8):
        state = level(state, ids(labels, number), tables, mats, BITS[number])
    quarter = ROWS // 2
    tails = []
    done = [dot(order[ROWS:], half.astype(bf16)) for half in state]
    for kept in range(2):
        for half in range(2):
            column = done[half][kept * quarter : (kept + 1) * quarter]
            for plane in range(2):
                rows_ref[pl.ds(4 * kept + 2 * half + plane, quarter, stride=14), :] = column[
                    :, plane * KP : plane * KP + 128
                ]
                tails.append(column[:, plane * KP + 128 : (plane + 1) * KP])
    for row in range(6):
        part = row % 3
        guest = jnp.where(tail_lanes(part), tails[6 + row // 3], 0.0)
        guest = pltpu.roll(guest, TAIL - part * ROOM, 1)
        rows_ref[pl.ds(8 + row, quarter, stride=14), :] = tails[row] + guest
    out_ref[...] = rows_ref[...].astype(bf16)


VMEM = pl.BlockSpec(memory_space=pltpu.VMEM)
SMEM = pl.BlockSpec(memory_space=pltpu.SMEM)
GRANT = pltpu.CompilerParams(vmem_limit_bytes=20 * 2**20)


def open_levels(side, got, tables, mats):
    half = jax.ShapeDtypeStruct((ROWS, 2 * KP), bf16)
    return pl.pallas_call(
        opening,
        out_shape=(half, half, jax.ShapeDtypeStruct((ROWS, 128), bf16)),
        in_specs=[SMEM] + [VMEM] * 3,
        out_specs=(VMEM, VMEM, VMEM),
        scratch_shapes=[pltpu.VMEM((2048, 128), f32)],
        compiler_params=GRANT,
        name="opening",
    )(side, got, tables, mats)


def close_levels(side, keep, got, labels, tables, mats, order):
    return pl.pallas_call(
        closing,
        out_shape=jax.ShapeDtypeStruct((1792, 128), bf16),
        in_specs=[SMEM] + [VMEM] * 6,
        out_specs=VMEM,
        scratch_shapes=[pltpu.VMEM((1792, 128), f32)],
        compiler_params=GRANT,
        name="closing",
    )(side, keep, got, labels, tables, mats, order)


def across(a, b):
    return lax.dot_general(a, b, (((1,), (1,)), ((), ())), preferred_element_type=f32)


def same_lane():
    here = lax.broadcasted_iota(jnp.int32, (128, 128), 0)
    there = lax.broadcasted_iota(jnp.int32, (128, 128), 1)
    return jnp.where(here == there, 1.0, 0.0).astype(bf16)


def pack(weights_ref, ids_ref, out_ref, rows_ref):
    tags = ids_ref[...].astype(f32)
    same = same_lane()
    for half in range(2):
        for kept in range(2):
            start = half * ROWS + kept * 128
            labels = jnp.concatenate(
                [
                    tags[1:, kept * 128 : (kept + 1) * 128],
                    tags[1:, ROWS + kept * 128 : ROWS + (kept + 1) * 128],
                    jnp.broadcast_to(tags[:1, start : start + 128], (KP - K - 16, 128)),
                ],
                axis=0,
            )
            first = jnp.concatenate(
                [weights_ref[0, :, start : start + 128].astype(f32), labels], axis=0
            ).astype(bf16)
            first = across(same, first)
            second = across(same, weights_ref[1, :, start : start + 128])
            pieces = [
                first[:, :128],
                first[:, 128:],
                second[:, :128],
                jnp.concatenate([second[:, 128:], jnp.zeros((128, KP - K), f32)], axis=1),
            ]
            for part, piece in enumerate(pieces):
                for y in range(4):
                    rows_ref[
                        pl.ds((2 * y + half) * 256 + 4 * kept + part, 32, stride=8), :
                    ] = piece[32 * y : 32 * (y + 1)]
    out_ref[...] = rows_ref[...].astype(bf16)


def pack_columns(weights, box_ids):
    return pl.pallas_call(
        pack,
        out_shape=jax.ShapeDtypeStruct((2048, 128), bf16),
        in_specs=[VMEM] * 2,
        out_specs=VMEM,
        scratch_shapes=[pltpu.VMEM((2048, 128), f32)],
        name="pack",
    )(weights, box_ids)


def unpack(back_ref, out_ref, rows_ref):
    rows_ref[...] = back_ref[...].astype(f32)
    same = same_lane()
    count = ROWS // 2
    shared = [rows_ref[pl.ds(8 + row, count, stride=14), :] for row in range(6)]
    tails = list(shared)
    for group in range(2):
        guest = jnp.zeros((count, 128), f32)
        for part in range(3):
            moved = pltpu.roll(shared[3 * group + part], 128 - TAIL + part * ROOM, 1)
            guest = jnp.where(tail_lanes(part), moved, guest)
        tails.append(guest)
    for kept in range(2):
        for half in range(2):
            for plane in range(2):
                number = 4 * kept + 2 * half + plane
                head = rows_ref[pl.ds(number, count, stride=14), :]
                block = jnp.concatenate(
                    [
                        across(same, head.astype(bf16)),
                        across(same, tails[number].astype(bf16))[:TAIL],
                    ],
                    axis=0,
                )
                start = half * ROWS + kept * 128
                out_ref[plane, :, start : start + 128] = block.astype(bf16)


def unpack_columns(back):
    return pl.pallas_call(
        unpack,
        out_shape=jax.ShapeDtypeStruct((2, K, 512), bf16),
        in_specs=[VMEM],
        out_specs=VMEM,
        scratch_shapes=[pltpu.VMEM((1792, 128), f32)],
        compiler_params=GRANT,
        name="unpack",
    )(back)


def row_order():
    row = jnp.arange(ROWS)
    moved = (row & 31) * 8 + (row >> 5)
    there = (moved[:, None] == row[None, :]).astype(bf16)
    return jnp.concatenate([there, there.T], axis=0)


def pack_tables(angles):
    wide = jnp.pad(jnp.stack([jnp.cos(angles), jnp.sin(angles)]), ((0, 0), (0, KP - K), (0, 0)))
    return wide.transpose(2, 0, 1).reshape(256, 2 * KP).astype(bf16)


def pack_mats(translate):
    wide = jnp.pad(translate, ((0, 0), (0, 0), (0, KP - K), (0, KP - K)))
    return wide.transpose(1, 3, 0, 2).reshape(2 * KP, 2 * KP)


def shards(weights, translate, angles, box_ids):
    packed = pack_columns(weights, box_ids).reshape(256, 8, 128)
    got = lax.all_to_all(packed, OUT, 0, 0, tiled=True).reshape(2048, 128)
    side = jnp.stack([lax.axis_index("zh"), lax.axis_index("core")])
    tables, mats = pack_tables(angles), pack_mats(translate)
    keep, send, labels = open_levels(side, got, tables, mats)
    far = lax.ppermute(send, "core", [(0, 1), (1, 0)])
    out = close_levels(side, keep, far, labels, tables, mats, row_order())
    back = lax.all_to_all(out.reshape(128, 7, 2, 128), BACK, 0, 0, tiled=True)
    return unpack_columns(back.reshape(1792, 128))


def solution(mesh):
    grid = Mesh(mesh.devices.reshape(4, 2, 4, 2, 8), AXES)
    columns = P(None, None, AXES)
    return jax.shard_map(
        shards,
        mesh=grid,
        in_specs=(columns, P(), P(), P(None, AXES)),
        out_specs=columns,
        check_vma=False,
    )
```

time: 110 us -> 108 us (0.982)
  starting transfers between devices: 24.3 us -> 31.4 us
  blocking collectives: 40.7 us -> 35 us
  waiting for transfers between devices: 33.4 us -> 28.9 us
  Pallas kernels: 8.66 us -> 10.2 us
    ppermute x0 -> x1, starting transfers between devices: none -> 5.98 us  [shards(): far = lax.ppermute(send, 'core', [(0, 1), (1, 0)])]
    all_to_all x1, blocking collectives: 40.7 us -> 35 us  [shards(): back = lax.all_to_all(out.reshape(128, 7, 2, 128), BACK, 0, 0, tiled=True)]
    all_to_all x1, waiting for transfers between devices: 33.4 us -> 27.9 us  [shards(): got = lax.all_to_all(packed, OUT, 0, 0, tiled=True).reshape(2048, 128)]
    pallas_call x1 -> x2, Pallas kernels: 5.18 us -> 6.65 us  [the longest x1 4.05 us: close_levels(): pl.pallas_call(closing, out_shape=jax.ShapeDtypeStruct((1792, 128), bf16)...]
    all_to_all x1, starting transfers between devices: 24.3 us -> 25.5 us  [shards(): got = lax.all_to_all(packed, OUT, 0, 0, tiled=True).reshape(2048, 128)]
  transfers between devices with their start and end apart: 1 -> 2, of which waited for: 1 -> 2; matrix products, arithmetic and copies ran while one was open for 2% -> 2% of each run, Pallas kernels for 0% -> 0%
where the time goes in v3:
time: 108 us
  blocking collectives  35 us (32%)
  starting transfers between devices  31.4 us (29%)
  waiting for transfers between devices  28.9 us (27%)
  Pallas kernels  10.2 us (9%)
  local copies, waits for them, and re-layouts  1.58 us (1%)
    all_to_all x1, blocking collectives, shards(): back = lax.all_to_all(out.reshape(128, 7, 2, 128), BACK, 0, 0, tiled=True)  35 us
    all_to_all x1, waiting for transfers between devices, shards(): got = lax.all_to_all(packed, OUT, 0, 0, tiled=True).reshape(2048, 128)  27.9 us
    all_to_all x1, starting transfers between devices, shards(): got = lax.all_to_all(packed, OUT, 0, 0, tiled=True).reshape(2048, 128)  25.5 us
    ppermute x1, starting transfers between devices, shards(): far = lax.ppermute(send, 'core', [(0, 1), (1, 0)])  5.98 us
    pallas_call x1, Pallas kernels, close_levels(): pl.pallas_call(closing, out_shape=jax.ShapeDtypeStruct((1792, 128), bf16)...  4.05 us
    pallas_call x1, Pallas kernels, open_levels(): pl.pallas_call(opening, out_shape=(half, half, jax.ShapeDtypeStruct((ROWS...  2.6 us
    pallas_call x1, Pallas kernels, pack_columns(): pl.pallas_call(pack, out_shape=jax.ShapeDtypeStruct((2048, 128), bf16), i...  2.22 us
  transfers between devices with their start and end apart: 2, of which 2 were waited for; matrix products, arithmetic and copies ran while one was open for 2% of the time, Pallas kernels for 0%

profile of v3, /device:TPU:1, one launch (start us, length us, event | category | flops | bytes accessed | tf_op | source)
XLA Modules:
  0.0 108.2 jit_solution(12480200027098352795)
XLA Ops:
  0.0 2.2 %pack.1 = bf16[2048,128]{1,0:T(8,128)(2,1)} custom-call(bf16[2,216,512]{2,1,0:T(8,128)(2,1)} %weights_ref.1, s32[9,512]{1,0:T(8,128)} %ids_ref.1), custom_call_target="tpu_custom_call" | custom-call | tf_op jit(solution)/shard_map/pack/pallas_call | solution.py:253
  2.2 0.0 copy-start.1
  2.2 25.5 %all-to-all-start = ((bf16[256,8,128]{2,1,0:T(8,128)(2,1)}), bf16[256,8,128]{2,1,0:T(8,128)(2,1)S(1)}, u32[]{:S(2)}, u32[]{:S(2)}) async-start(bf16[256,8,128]{2,1,0:T(8,128)(2,1)} %bitcast.23), calls=%async_computation | async-start | bytes 1048576 | tf_op jit(solution)/shard_map/all_to_all | solution.py:322
  27.7 0.0 copy-done.1
  27.7 0.8 fusion.3
  28.5 0.0 copy-start
  28.5 0.1 copy.7.tab_ref
  28.7 0.8 copy-done
  29.5 0.1 pad_bitcast_fusion
  29.6 0.5 copy.6
  30.1 0.1 copy.8
  30.1 0.1 pad_add_fusion.side_ref
  30.2 27.9 %all-to-all-done = bf16[256,8,128]{2,1,0:T(8,128)(2,1)S(1)} async-done(((bf16[256,8,128]{2,1,0:T(8,128)(2,1)}), bf16[256,8,128]{2,1,0:T(8,128)(2,1)S(1)}, u32[]{:S(2)}, u32[]{:S(2)}) %all-to-all-start) | async-done | bytes 524320 | tf_op jit(solution)/shard_map/all_to_all | solution.py:322
  58.1 2.6 %opening.1 = (bf16[256,512]{1,0:T(8,128)(2,1)S(1)}, bf16[256,512]{1,0:T(8,128)(2,1)S(1)}, bf16[256,128]{1,0:T(8,128)(2,1)S(1)}) custom-call(s32[2]{0:T(128)S(1)} %pad_add_fusion.side_ref, bf16[2048,128]{1,0:T(8,128)(2,1)S(1)} %bitcast.20, bf16[256,512]{1,0:T(8,128)(2,1)S(1)} %copy.7.tab_ref, bf16[512,512]{1,0:T(8,128)(2,1)S(1)} %bitcast.18), custom_call_target="tpu_custom_call" | custom-call | tf_op jit(solution)/shard_map/opening/pallas_call | solution.py:186
  60.7 6.0 %collective-permute-start = (bf16[256,512]{1,0:T(8,128)(2,1)S(1)}, bf16[256,512]{1,0:T(8,128)(2,1)S(1)}, u32[]{:S(2)}, u32[]{:S(2)}) collective-permute-start(bf16[256,512]{1,0:T(8,128)(2,1)S(1)} %get-tuple-element.9), channel_id=1, source_target_pairs={{0,8},{8,0},{1,9},{9,1},{2,10},{10,2},{3,11},{11,3},{4,12},{12,4},... | collective-permute-start | bytes 786440 | tf_op jit(solution)/shard_map/ppermute | solution.py:326
  66.7 0.1 iota_compare_fusion.2
  66.9 1.0 collective-permute-done.got_ref
  67.9 4.0 %closing.1 = bf16[1792,128]{1,0:T(8,128)(2,1)S(1)} custom-call(s32[2]{0:T(128)S(1)} %pad_add_fusion.side_ref, bf16[256,512]{1,0:T(8,128)(2,1)S(1)} %get-tuple-element.8.keep_ref, bf16[256,512]{1,0:T(8,128)(2,1)S(1)} %collective-permute-done.got_ref, bf16[256,128]{1,0:T(8,128)(2,1)S(1)} %get-tuple-element.10.label_ref, bf16[256,512]{1,0:T(8,128)(2,1)S(1)} %copy.7.tab_ref, ...), custom_call_target="tpu_custom_call" | custom-call | tf_op jit(solution)/shard_map/closing/pallas_call | solution.py:198
  71.9 35.0 %all_to_all.10 = bf16[128,7,2,128]{3,2,1,0:T(2,128)(2,1)S(1)} all-to-all(bf16[128,7,2,128]{3,2,1,0:T(2,128)(2,1)S(1)} %bitcast.21), channel_id=1, replica_groups=mesh['y'=4,'zh'=2,'x'=4,'core'=2,'zl'=8] {'y','x','zl'}, dimensions={0} | all-to-all | bytes 917504 | tf_op jit(solution)/shard_map/all_to_all | solution.py:328
  106.9 1.3 %unpack.1 = bf16[2,216,512]{2,1,0:T(8,128)(2,1)} custom-call(bf16[1792,128]{1,0:T(8,128)(2,1)S(1)} %bitcast.22), custom_call_target="tpu_custom_call" | custom-call | tf_op jit(solution)/shard_map/unpack/pallas_call | solution.py:292
  (3 shorter events, 0.1 us)
Async XLA Ops:
  2.2 25.5 %copy-start.1 = (f32[216,256]{1,0:T(8,128)S(1)}, f32[216,256]{1,0:T(8,128)}, u32[]{:S(2)}) copy-start(f32[216,256]{1,0:T(8,128)} %param.6) | copy-start | bytes 663556
  2.2 55.9 %all-to-all-start = ((bf16[256,8,128]{2,1,0:T(8,128)(2,1)}), bf16[256,8,128]{2,1,0:T(8,128)(2,1)S(1)}, u32[]{:S(2)}, u32[]{:S(2)}) async-start(bf16[256,8,128]{2,1,0:T(8,128)(2,1)} %bitcast.23), calls=%async_computation | async-start | bytes 1048576 | tf_op jit(solution)/shard_map/all_to_all | solution.py:322
  28.5 1.0 copy-start
  60.7 7.1 %collective-permute-start = (bf16[256,512]{1,0:T(8,128)(2,1)S(1)}, bf16[256,512]{1,0:T(8,128)(2,1)S(1)}, u32[]{:S(2)}, u32[]{:S(2)}) collective-permute-start(bf16[256,512]{1,0:T(8,128)(2,1)S(1)} %get-tuple-element.9), channel_id=1, source_target_pairs={{0,8},{8,0},{1,9},{9,1},{2,10},{10,2},{3,11},{11,3},{4,12},{12,4},... | collective-permute-start | bytes 786440 | tf_op jit(solution)/shard_map/ppermute | solution.py:326

commit v4 on v3

--- a/solution.py
+++ b/solution.py
@@ -11,8 +11,8 @@
 ROWS = 256
 LEVELS = 9
 AXES = ("y", "zh", "x", "core", "zl")
-OUT = ("y", "zh", "x", "zl")
-BACK = ("y", "x", "zl")
+OUT = ("zh", "zl", "y", "x")
+BACK = ("zl", "y", "x")
 ID_LANE = K + 16
 TAIL = K - 128
 ROOM = 128 - TAIL
@@ -75,7 +75,7 @@
     return values.astype(bf16).astype(f32)
 
 
-def opening(side_ref, got_ref, tab_ref, mat_ref, keep_ref, send_ref, label_ref, rows_ref):
+def opening(side_ref, got_ref, tab_ref, mat_ref, order_ref, keep_ref, send_ref, label_ref, rows_ref):
     tables = tab_ref[...]
     mats = mat_ref[...]
     quarter = ROWS // 2
@@ -85,10 +85,11 @@
         got = jnp.concatenate(
             [rows_ref[pl.ds(4 * kept + part, ROWS, stride=8), :] for part in range(4)], axis=1
         )
+        got = dot(order_ref[...], got.astype(bf16))
         re, im = turn(got[:, ID_LANE : ID_LANE + 1], got, tables)
-        stacked += [split(re, 32), split(im, 32)]
-        tags = got[:, 128:256].reshape(4, 2, 32, 128)
-        labels.append(jnp.where(side_ref[0] == 0, tags[:, 0], tags[:, 1]).reshape(quarter, 128))
+        stacked += [split(re, quarter), split(im, quarter)]
+        tags = got[:, 128:256]
+        labels.append(jnp.where(side_ref[0] == 0, tags[:quarter], tags[quarter:]))
     labels = jnp.concatenate(labels, axis=0)
     mixed = dot(jnp.concatenate(stacked, axis=0), mats)
     state = []
@@ -153,16 +154,16 @@
     for number in (4, 5):
         state = level(state, ids(labels, number), tables, mats, BITS[number])
     order = order_ref[...]
-    labels = dot(order[:ROWS], labels.astype(bf16))
-    state = [dot(order[:ROWS], half.astype(bf16)) for half in state]
+    labels = dot(order, labels.astype(bf16))
+    state = [dot(order, half.astype(bf16)) for half in state]
     for number in (6, 7, 8):
         state = level(state, ids(labels, number), tables, mats, BITS[number])
     quarter = ROWS // 2
     tails = []
-    done = [dot(order[ROWS:], half.astype(bf16)) for half in state]
+    done = [half.reshape(8, 2, 16, 2 * KP) for half in state]
     for kept in range(2):
         for half in range(2):
-            column = done[half][kept * quarter : (kept + 1) * quarter]
+            column = done[half][:, kept].reshape(quarter, 2 * KP)
             for plane in range(2):
                 rows_ref[pl.ds(4 * kept + 2 * half + plane, quarter, stride=14), :] = column[
                     :, plane * KP : plane * KP + 128
@@ -181,17 +182,17 @@
 GRANT = pltpu.CompilerParams(vmem_limit_bytes=20 * 2**20)
 
 
-def open_levels(side, got, tables, mats):
+def open_levels(side, got, tables, mats, order):
     half = jax.ShapeDtypeStruct((ROWS, 2 * KP), bf16)
     return pl.pallas_call(
         opening,
         out_shape=(half, half, jax.ShapeDtypeStruct((ROWS, 128), bf16)),
-        in_specs=[SMEM] + [VMEM] * 3,
+        in_specs=[SMEM] + [VMEM] * 4,
         out_specs=(VMEM, VMEM, VMEM),
         scratch_shapes=[pltpu.VMEM((2048, 128), f32)],
         compiler_params=GRANT,
         name="opening",
-    )(side, got, tables, mats)
+    )(side, got, tables, mats, order)
 
 
 def close_levels(side, keep, got, labels, tables, mats, order):
@@ -216,48 +217,48 @@
     return jnp.where(here == there, 1.0, 0.0).astype(bf16)
 
 
-def pack(weights_ref, ids_ref, out_ref, rows_ref):
-    tags = ids_ref[...].astype(f32)
+def pack(weights_ref, ids_ref, all_ids_ref, out_ref, rows_ref):
+    own = ids_ref[...].astype(f32)
+    tags = all_ids_ref[...].astype(f32)
     same = same_lane()
-    for half in range(2):
-        for kept in range(2):
-            start = half * ROWS + kept * 128
-            labels = jnp.concatenate(
-                [
-                    tags[1:, kept * 128 : (kept + 1) * 128],
-                    tags[1:, ROWS + kept * 128 : ROWS + (kept + 1) * 128],
-                    jnp.broadcast_to(tags[:1, start : start + 128], (KP - K - 16, 128)),
-                ],
-                axis=0,
-            )
-            first = jnp.concatenate(
-                [weights_ref[0, :, start : start + 128].astype(f32), labels], axis=0
-            ).astype(bf16)
-            first = across(same, first)
-            second = across(same, weights_ref[1, :, start : start + 128])
-            pieces = [
-                first[:, :128],
-                first[:, 128:],
-                second[:, :128],
-                jnp.concatenate([second[:, 128:], jnp.zeros((128, KP - K), f32)], axis=1),
-            ]
-            for part, piece in enumerate(pieces):
-                for y in range(4):
-                    rows_ref[
-                        pl.ds((2 * y + half) * 256 + 4 * kept + part, 32, stride=8), :
-                    ] = piece[32 * y : 32 * (y + 1)]
+    for kept in range(2):
+        lanes = slice(kept * 128, (kept + 1) * 128)
+        labels = jnp.concatenate(
+            [
+                tags[1:, lanes],
+                tags[1:, ROWS + kept * 128 : ROWS + (kept + 1) * 128],
+                jnp.broadcast_to(own[:1, lanes], (KP - K - 16, 128)),
+            ],
+            axis=0,
+        )
+        first = jnp.concatenate([weights_ref[0, :, lanes].astype(f32), labels], axis=0)
+        first = across(same, first.astype(bf16))
+        second = across(same, weights_ref[1, :, lanes])
+        pieces = [
+            first[:, :128],
+            first[:, 128:],
+            second[:, :128],
+            jnp.concatenate([second[:, 128:], jnp.zeros((128, KP - K), f32)], axis=1),
+        ]
+        for part, piece in enumerate(pieces):
+            rows_ref[pl.ds(4 * kept + part, 128, stride=8), :] = piece
     out_ref[...] = rows_ref[...].astype(bf16)
 
 
 def pack_columns(weights, box_ids):
     return pl.pallas_call(
         pack,
+        grid=(2,),
         out_shape=jax.ShapeDtypeStruct((2048, 128), bf16),
-        in_specs=[VMEM] * 2,
-        out_specs=VMEM,
-        scratch_shapes=[pltpu.VMEM((2048, 128), f32)],
+        in_specs=[
+            pl.BlockSpec((2, K, ROWS), lambda half: (0, 0, half)),
+            pl.BlockSpec((LEVELS, ROWS), lambda half: (0, half)),
+            pl.BlockSpec((LEVELS, 2 * ROWS), lambda half: (0, 0)),
+        ],
+        out_specs=pl.BlockSpec((1024, 128), lambda half: (half, 0)),
+        scratch_shapes=[pltpu.VMEM((1024, 128), f32)],
         name="pack",
-    )(weights, box_ids)
+    )(weights, box_ids, box_ids)
 
 
 def unpack(back_ref, out_ref, rows_ref):
@@ -300,11 +301,14 @@
     )(back)
 
 
-def row_order():
+def one_hot(source):
+    return (source[:, None] == jnp.arange(ROWS)[None, :]).astype(bf16)
+
+
+def row_orders():
     row = jnp.arange(ROWS)
-    moved = (row & 31) * 8 + (row >> 5)
-    there = (moved[:, None] == row[None, :]).astype(bf16)
-    return jnp.concatenate([there, there.T], axis=0)
+    enter = one_hot((row & 128) + (row & 7) * 16 + ((row >> 3) & 15))
+    return enter, one_hot((row & 31) * 8 + (row >> 5))
 
 
 def pack_tables(angles):
@@ -322,9 +326,10 @@
     got = lax.all_to_all(packed, OUT, 0, 0, tiled=True).reshape(2048, 128)
     side = jnp.stack([lax.axis_index("zh"), lax.axis_index("core")])
     tables, mats = pack_tables(angles), pack_mats(translate)
-    keep, send, labels = open_levels(side, got, tables, mats)
+    enter, order = row_orders()
+    keep, send, labels = open_levels(side, got, tables, mats, enter)
     far = lax.ppermute(send, "core", [(0, 1), (1, 0)])
-    out = close_levels(side, keep, far, labels, tables, mats, row_order())
+    out = close_levels(side, keep, far, labels, tables, mats, order)
     back = lax.all_to_all(out.reshape(128, 7, 2, 128), BACK, 0, 0, tiled=True)
     return unpack_columns(back.reshape(1792, 128))
 

time: 108 us -> 108 us (level); the launches traced: 108 us -> 107 us
  blocking collectives: 35 us -> 33.5 us
    all_to_all x1, blocking collectives: 35 us -> 33.5 us  [shards(): back = lax.all_to_all(out.reshape(128, 7, 2, 128), BACK, 0, 0, tiled=True)]
where the time goes in v4:
time: 108 us; the launch traced here: 107 us
  blocking collectives  33.5 us (31%)
  starting transfers between devices  30.7 us (28%)
  waiting for transfers between devices  29.7 us (28%)
  Pallas kernels  10.1 us (9%)
  local copies, waits for them, and re-layouts  1.58 us (1%)
  other arithmetic  1.1 us (1%)
    all_to_all x1, blocking collectives, shards(): back = lax.all_to_all(out.reshape(128, 7, 2, 128), BACK, 0, 0, tiled=True)  33.5 us
    all_to_all x1, waiting for transfers between devices, shards(): got = lax.all_to_all(packed, OUT, 0, 0, tiled=True).reshape(2048, 128)  28.7 us
    all_to_all x1, starting transfers between devices, shards(): got = lax.all_to_all(packed, OUT, 0, 0, tiled=True).reshape(2048, 128)  25.5 us
    ppermute x1, starting transfers between devices, shards(): far = lax.ppermute(send, 'core', [(0, 1), (1, 0)])  5.22 us
    pallas_call x1, Pallas kernels, close_levels(): pl.pallas_call(closing, out_shape=jax.ShapeDtypeStruct((1792, 128), bf16)...  3.77 us
    pallas_call x1, Pallas kernels, open_levels(): pl.pallas_call(opening, out_shape=(half, half, jax.ShapeDtypeStruct((ROWS...  2.8 us
    pallas_call x1, Pallas kernels, pack_columns(): pl.pallas_call(pack, grid=(2,), out_shape=jax.ShapeDtypeStruct((2048, 128...  2.25 us
  transfers between devices with their start and end apart: 2, of which 2 were waited for; matrix products, arithmetic and copies ran while one was open for 2% of the time, Pallas kernels for 0%

profile of v4, /device:TPU:1, one launch (start us, length us, event | category | flops | bytes accessed | tf_op | source)
XLA Modules:
  0.0 106.8 jit_solution(10832889805928719286)
XLA Ops:
  0.0 2.2 %pack.1 = bf16[2048,128]{1,0:T(8,128)(2,1)} custom-call(bf16[2,216,512]{2,1,0:T(8,128)(2,1)} %weights_ref.1, s32[9,512]{1,0:T(8,128)} %all_ids_ref.1, s32[9,512]{1,0:T(8,128)} %all_ids_ref.1), custom_call_target="tpu_custom_call" | custom-call | tf_op jit(solution)/shard_map/pack/pallas_call | solution.py:249
  2.3 0.0 copy-start.1
  2.3 25.5 %all-to-all-start = ((bf16[256,8,128]{2,1,0:T(8,128)(2,1)}), bf16[256,8,128]{2,1,0:T(8,128)(2,1)S(1)}, u32[]{:S(2)}, u32[]{:S(2)}) async-start(bf16[256,8,128]{2,1,0:T(8,128)(2,1)} %bitcast.23), calls=%async_computation | async-start | bytes 1048576 | tf_op jit(solution)/shard_map/all_to_all | solution.py:326
  27.7 0.0 copy-done.1
  27.7 0.8 fusion.5
  28.5 0.0 copy-start
  28.6 0.1 copy.7.tab_ref
  28.7 0.8 copy-done
  29.6 0.1 pad_bitcast_fusion
  29.6 0.5 copy.6
  30.1 0.1 copy.8
  30.2 0.1 pad_add_fusion.side_ref
  30.3 0.1 fusion.3.order_ref
  30.4 28.7 %all-to-all-done = bf16[256,8,128]{2,1,0:T(8,128)(2,1)S(1)} async-done(((bf16[256,8,128]{2,1,0:T(8,128)(2,1)}), bf16[256,8,128]{2,1,0:T(8,128)(2,1)S(1)}, u32[]{:S(2)}, u32[]{:S(2)}) %all-to-all-start) | async-done | bytes 524320 | tf_op jit(solution)/shard_map/all_to_all | solution.py:326
  59.0 2.8 %opening.1 = (bf16[256,512]{1,0:T(8,128)(2,1)S(1)}, bf16[256,512]{1,0:T(8,128)(2,1)S(1)}, bf16[256,128]{1,0:T(8,128)(2,1)S(1)}) custom-call(s32[2]{0:T(128)S(1)} %pad_add_fusion.side_ref, bf16[2048,128]{1,0:T(8,128)(2,1)S(1)} %bitcast.20, bf16[256,512]{1,0:T(8,128)(2,1)S(1)} %copy.7.tab_ref, bf16[512,512]{1,0:T(8,128)(2,1)S(1)} %bitcast.18, ...), custom_call_target="tpu_custom_call" | custom-call | tf_op jit(solution)/shard_map/opening/pallas_call | solution.py:187
  61.8 5.2 %collective-permute-start = (bf16[256,512]{1,0:T(8,128)(2,1)S(1)}, bf16[256,512]{1,0:T(8,128)(2,1)S(1)}, u32[]{:S(2)}, u32[]{:S(2)}) collective-permute-start(bf16[256,512]{1,0:T(8,128)(2,1)S(1)} %get-tuple-element.9), channel_id=1, source_target_pairs={{0,8},{8,0},{1,9},{9,1},{2,10},{10,2},{3,11},{11,3},{4,12},{12,4},... | collective-permute-start | bytes 786440 | tf_op jit(solution)/shard_map/ppermute | solution.py:331
  67.1 0.1 fusion.4.order_ref
  67.2 1.0 collective-permute-done.got_ref
  68.2 3.8 %closing.1 = bf16[1792,128]{1,0:T(8,128)(2,1)S(1)} custom-call(s32[2]{0:T(128)S(1)} %pad_add_fusion.side_ref, bf16[256,512]{1,0:T(8,128)(2,1)S(1)} %get-tuple-element.8.keep_ref, bf16[256,512]{1,0:T(8,128)(2,1)S(1)} %collective-permute-done.got_ref, bf16[256,128]{1,0:T(8,128)(2,1)S(1)} %get-tuple-element.10.label_ref, bf16[256,512]{1,0:T(8,128)(2,1)S(1)} %copy.7.tab_ref, ...), custom_call_target="tpu_custom_call" | custom-call | tf_op jit(solution)/shard_map/closing/pallas_call | solution.py:199
  72.0 33.5 %all_to_all.10 = bf16[128,7,2,128]{3,2,1,0:T(2,128)(2,1)S(1)} all-to-all(bf16[128,7,2,128]{3,2,1,0:T(2,128)(2,1)S(1)} %bitcast.22), channel_id=1, replica_groups=mesh['y'=4,'zh'=2,'x'=4,'core'=2,'zl'=8] {'zl','y','x'}, dimensions={0} | all-to-all | bytes 917504 | tf_op jit(solution)/shard_map/all_to_all | solution.py:333
  105.5 1.3 %unpack.1 = bf16[2,216,512]{2,1,0:T(8,128)(2,1)} custom-call(bf16[1792,128]{1,0:T(8,128)(2,1)S(1)} %bitcast.21), custom_call_target="tpu_custom_call" | custom-call | tf_op jit(solution)/shard_map/unpack/pallas_call | solution.py:293
  (3 shorter events, 0.0 us)
Async XLA Ops:
  2.3 25.5 %copy-start.1 = (f32[216,256]{1,0:T(8,128)S(1)}, f32[216,256]{1,0:T(8,128)}, u32[]{:S(2)}) copy-start(f32[216,256]{1,0:T(8,128)} %param.6) | copy-start | bytes 663556
  2.3 56.8 %all-to-all-start = ((bf16[256,8,128]{2,1,0:T(8,128)(2,1)}), bf16[256,8,128]{2,1,0:T(8,128)(2,1)S(1)}, u32[]{:S(2)}, u32[]{:S(2)}) async-start(bf16[256,8,128]{2,1,0:T(8,128)(2,1)} %bitcast.23), calls=%async_computation | async-start | bytes 1048576 | tf_op jit(solution)/shard_map/all_to_all | solution.py:326
  28.5 1.0 copy-start
  61.8 6.4 %collective-permute-start = (bf16[256,512]{1,0:T(8,128)(2,1)S(1)}, bf16[256,512]{1,0:T(8,128)(2,1)S(1)}, u32[]{:S(2)}, u32[]{:S(2)}) collective-permute-start(bf16[256,512]{1,0:T(8,128)(2,1)S(1)} %get-tuple-element.9), channel_id=1, source_target_pairs={{0,8},{8,0},{1,9},{9,1},{2,10},{10,2},{3,11},{11,3},{4,12},{12,4},... | collective-permute-start | bytes 786440 | tf_op jit(solution)/shard_map/ppermute | solution.py:331

commit v5 on v4

--- a/solution.py
+++ b/solution.py
@@ -16,6 +16,7 @@
 ID_LANE = K + 16
 TAIL = K - 128
 ROOM = 128 - TAIL
+AHEAD = (4, 5, 6, 7, 8)
 BITS = {1: 5, 2: 6, 4: 3, 5: 4, 6: 5, 7: 6, 8: 7}
 f32 = jnp.float32
 bf16 = jnp.bfloat16
@@ -25,10 +26,12 @@
     return jnp.dot(a, b, preferred_element_type=f32)
 
 
-def turn(ids, state, tables):
-    rows = ids.shape[0]
-    boxes = lax.broadcasted_iota(jnp.int32, (rows, KP), 1).astype(f32)
-    picked = dot(jnp.where(ids == boxes, 1.0, 0.0).astype(bf16), tables)
+def look_up(ids, tables):
+    boxes = lax.broadcasted_iota(jnp.int32, (ids.shape[0], KP), 1).astype(f32)
+    return dot(jnp.where(ids == boxes, 1.0, 0.0).astype(bf16), tables)
+
+
+def turn(picked, state):
     cosines, sines = picked[:, :KP], picked[:, KP:]
     re, im = state[:, :KP], state[:, KP:]
     return cosines * re - sines * im, sines * re + cosines * im
@@ -42,11 +45,11 @@
     ).astype(bf16)
 
 
-def level(state, ids, tables, mats, bit):
+def level(state, picked, mats, bit):
     block = 1 << bit
     stacked = []
     for half in range(2):
-        re, im = turn(ids[half], state[half], tables)
+        re, im = turn(picked[half], state[half])
         stacked += [split(re, block), split(im, block)]
     mixed = dot(jnp.concatenate(stacked, axis=0), mats)
     quarter = ROWS // 2
@@ -71,6 +74,10 @@
     return [labels[:, first + 8 * half : first + 8 * half + 1] for half in range(2)]
 
 
+def both(labels, number, tables):
+    return [look_up(tags, tables) for tags in ids(labels, number)]
+
+
 def round_to(values):
     return values.astype(bf16).astype(f32)
 
@@ -86,7 +93,7 @@
             [rows_ref[pl.ds(4 * kept + part, ROWS, stride=8), :] for part in range(4)], axis=1
         )
         got = dot(order_ref[...], got.astype(bf16))
-        re, im = turn(got[:, ID_LANE : ID_LANE + 1], got, tables)
+        re, im = turn(look_up(got[:, ID_LANE : ID_LANE + 1], tables), got)
         stacked += [split(re, quarter), split(im, quarter)]
         tags = got[:, 128:256]
         labels.append(jnp.where(side_ref[0] == 0, tags[:quarter], tags[quarter:]))
@@ -108,9 +115,10 @@
             )
         )
     for number in (1, 2):
-        state = level(state, ids(labels, number), tables, mats, BITS[number])
+        state = level(state, both(labels, number, tables), mats, BITS[number])
+    picked = both(labels, 3, tables)
     turned = [
-        jnp.concatenate(turn(ids(labels, 3)[half], state[half], tables), axis=1).astype(bf16)
+        jnp.concatenate(turn(picked[half], state[half]), axis=1).astype(bf16)
         for half in range(2)
     ]
     low = side_ref[1] == 0
@@ -124,10 +132,28 @@
     return (lane >= part * ROOM) & (lane < (part + 1) * ROOM)
 
 
-def closing(side_ref, keep_ref, got_ref, label_ref, tab_ref, mat_ref, order_ref, out_ref, rows_ref):
+def lookup(label_ref, tab_ref, order_ref, out_ref):
+    tables = tab_ref[...]
+    early = label_ref[...].astype(f32)
+    late = dot(order_ref[...], label_ref[...])
+    for number in AHEAD:
+        picked = both(early if number < 6 else late, number, tables)
+        for half in range(2):
+            out_ref[2 * (number - AHEAD[0]) + half] = picked[half].astype(bf16)
+
+
+def closing(side_ref, keep_ref, got_ref, label_ref, picked_ref, tab_ref, mat_ref, order_ref, out_ref, rows_ref):
     tables = tab_ref[...]
     mats = mat_ref[...]
-    labels = label_ref[...].astype(f32)
+    order = order_ref[...]
+    late = dot(order, label_ref[...])
+
+    def angles_of(number):
+        if number not in AHEAD:
+            return both(late, number, tables)
+        first = 2 * (number - AHEAD[0])
+        return [picked_ref[first + half].astype(f32) for half in range(2)]
+
     flipped = jnp.concatenate([mats[KP:], mats[:KP]], axis=0)
     mixed = dot(
         jnp.concatenate(
@@ -152,12 +178,10 @@
         for target in range(2)
     ]
     for number in (4, 5):
-        state = level(state, ids(labels, number), tables, mats, BITS[number])
-    order = order_ref[...]
-    labels = dot(order, labels.astype(bf16))
+        state = level(state, angles_of(number), mats, BITS[number])
     state = [dot(order, half.astype(bf16)) for half in state]
     for number in (6, 7, 8):
-        state = level(state, ids(labels, number), tables, mats, BITS[number])
+        state = level(state, angles_of(number), mats, BITS[number])
     quarter = ROWS // 2
     tails = []
     done = [half.reshape(8, 2, 16, 2 * KP) for half in state]
@@ -195,16 +219,33 @@
     )(side, got, tables, mats, order)
 
 
-def close_levels(side, keep, got, labels, tables, mats, order):
+def look_ahead(labels, tables, order):
+    count = 2 * len(AHEAD)
+    return pl.pallas_call(
+        lookup,
+        out_shape=jax.ShapeDtypeStruct((count, ROWS, 2 * KP), bf16),
+        in_specs=[VMEM] * 3,
+        out_specs=VMEM,
+        compiler_params=GRANT,
+        cost_estimate=pl.CostEstimate(
+            flops=2 * count * ROWS * ROWS * 2 * KP,
+            bytes_accessed=2 * count * ROWS * 2 * KP,
+            transcendentals=0,
+        ),
+        name="lookup",
+    )(labels, tables, order)
+
+
+def close_levels(side, keep, got, labels, picked, tables, mats, order):
     return pl.pallas_call(
         closing,
         out_shape=jax.ShapeDtypeStruct((1792, 128), bf16),
-        in_specs=[SMEM] + [VMEM] * 6,
+        in_specs=[SMEM] + [VMEM] * 7,
         out_specs=VMEM,
         scratch_shapes=[pltpu.VMEM((1792, 128), f32)],
         compiler_params=GRANT,
         name="closing",
-    )(side, keep, got, labels, tables, mats, order)
+    )(side, keep, got, labels, picked, tables, mats, order)
 
 
 def across(a, b):
@@ -329,7 +370,8 @@
     enter, order = row_orders()
     keep, send, labels = open_levels(side, got, tables, mats, enter)
     far = lax.ppermute(send, "core", [(0, 1), (1, 0)])
-    out = close_levels(side, keep, far, labels, tables, mats, order)
+    picked = look_ahead(labels, tables, order)
+    out = close_levels(side, keep, far, labels, picked, tables, mats, order)
     back = lax.all_to_all(out.reshape(128, 7, 2, 128), BACK, 0, 0, tiled=True)
     return unpack_columns(back.reshape(1792, 128))
 

time: 108 us -> 108 us (level)
  transfers between devices with their start and end apart: 2 -> 2, of which waited for: 2 -> 2; matrix products, arithmetic and copies ran while one was open for 2% -> 3% of each run, Pallas kernels for 0% -> 1%
where the time goes in v5:
time: 108 us; the launch traced here: 107 us
  blocking collectives  33.5 us (31%)
  starting transfers between devices  30.5 us (28%)
  waiting for transfers between devices  28.7 us (27%)
  Pallas kernels  11 us (10%)
  other arithmetic  2.02 us (2%)
    all_to_all x1, blocking collectives, shards(): back = lax.all_to_all(out.reshape(128, 7, 2, 128), BACK, 0, 0, tiled=True)  33.5 us
    all_to_all x1, waiting for transfers between devices, shards(): got = lax.all_to_all(packed, OUT, 0, 0, tiled=True).reshape(2048, 128)  28.6 us
    all_to_all x1, starting transfers between devices, shards(): got = lax.all_to_all(packed, OUT, 0, 0, tiled=True).reshape(2048, 128)  25.3 us
    ppermute x1, starting transfers between devices, shards(): far = lax.ppermute(send, 'core', [(0, 1), (1, 0)])  5.19 us
    pallas_call x1, Pallas kernels, close_levels(): pl.pallas_call(closing, out_shape=jax.ShapeDtypeStruct((1792, 128), bf16)...  3.7 us
    pallas_call x1, Pallas kernels, open_levels(): pl.pallas_call(opening, out_shape=(half, half, jax.ShapeDtypeStruct((ROWS...  2.8 us
    pallas_call x1, Pallas kernels, pack_columns(): pl.pallas_call(pack, grid=(2,), out_shape=jax.ShapeDtypeStruct((2048, 128...  2.3 us
  transfers between devices with their start and end apart: 2, of which 2 were waited for; matrix products, arithmetic and copies ran while one was open for 3% of the time, Pallas kernels for 1%

profile of v5, /device:TPU:1, one launch (start us, length us, event | category | flops | bytes accessed | tf_op | source)
XLA Modules:
  0.0 106.6 jit_solution(97682382937856545)
XLA Ops:
  0.0 0.0 copy-start
  0.0 2.3 %pack.1 = bf16[2048,128]{1,0:T(8,128)(2,1)} custom-call(bf16[2,216,512]{2,1,0:T(8,128)(2,1)} %weights_ref.1, s32[9,512]{1,0:T(8,128)} %all_ids_ref.1, s32[9,512]{1,0:T(8,128)} %all_ids_ref.1), custom_call_target="tpu_custom_call" | custom-call | tf_op jit(solution)/shard_map/pack/pallas_call | solution.py:290
  2.3 25.3 %all-to-all-start = ((bf16[256,8,128]{2,1,0:T(8,128)(2,1)}), bf16[256,8,128]{2,1,0:T(8,128)(2,1)S(1)}, u32[]{:S(2)}, u32[]{:S(2)}) async-start(bf16[256,8,128]{2,1,0:T(8,128)(2,1)} %bitcast.23), calls=%async_computation | async-start | bytes 1048576 | tf_op jit(solution)/shard_map/all_to_all | solution.py:367
  27.7 1.7 %fusion.5 = (bf16[1,216,256]{2,1,0:T(8,128)(2,1)S(1)}, bf16[1,216,256]{2,1,0:T(8,128)(2,1)S(1)}) fusion(f32[216,256]{1,0:T(8,128)} %param.6), kind=kLoop, calls=%fused_computation.11 | loop fusion | flops 110592 | bytes 442368 | tf_op jit(solution)/shard_map/stack | solution.py:356
  29.4 0.1 copy.7.tab_ref
  29.5 0.0 copy-done
  29.6 0.1 pad_bitcast_fusion
  29.6 0.5 copy.6
  30.1 0.1 copy.8
  30.2 0.1 pad_add_fusion.side_ref
  30.3 0.1 fusion.3.order_ref
  30.4 28.6 %all-to-all-done = bf16[256,8,128]{2,1,0:T(8,128)(2,1)S(1)} async-done(((bf16[256,8,128]{2,1,0:T(8,128)(2,1)}), bf16[256,8,128]{2,1,0:T(8,128)(2,1)S(1)}, u32[]{:S(2)}, u32[]{:S(2)}) %all-to-all-start) | async-done | bytes 524320 | tf_op jit(solution)/shard_map/all_to_all | solution.py:367
  59.0 2.8 %opening.1 = (bf16[256,512]{1,0:T(8,128)(2,1)S(1)}, bf16[256,512]{1,0:T(8,128)(2,1)S(1)}, bf16[256,128]{1,0:T(8,128)(2,1)S(1)}) custom-call(s32[2]{0:T(128)S(1)} %pad_add_fusion.side_ref, bf16[2048,128]{1,0:T(8,128)(2,1)S(1)} %bitcast.20, bf16[256,512]{1,0:T(8,128)(2,1)S(1)} %copy.7.tab_ref, bf16[512,512]{1,0:T(8,128)(2,1)S(1)} %bitcast.18, ...), custom_call_target="tpu_custom_call" | custom-call | tf_op jit(solution)/shard_map/opening/pallas_call | solution.py:211
  61.8 5.2 %collective-permute-start = (bf16[256,512]{1,0:T(8,128)(2,1)S(1)}, bf16[256,512]{1,0:T(8,128)(2,1)S(1)}, u32[]{:S(2)}, u32[]{:S(2)}) collective-permute-start(bf16[256,512]{1,0:T(8,128)(2,1)S(1)} %get-tuple-element.9), channel_id=1, source_target_pairs={{0,8},{8,0},{1,9},{9,1},{2,10},{10,2},{3,11},{11,3},{4,12},{12,4},... | collective-permute-start | bytes 786440 | tf_op jit(solution)/shard_map/ppermute | solution.py:372
  67.0 0.1 fusion.4.order_ref
  67.1 0.9 lookup.1.picked_ref
  68.0 0.1 collective-permute-done.got_ref
  68.1 3.7 %closing.1 = bf16[1792,128]{1,0:T(8,128)(2,1)S(1)} custom-call(s32[2]{0:T(128)S(1)} %pad_add_fusion.side_ref, bf16[256,512]{1,0:T(8,128)(2,1)S(1)} %get-tuple-element.8.keep_ref, bf16[256,512]{1,0:T(8,128)(2,1)S(1)} %collective-permute-done.got_ref, bf16[256,128]{1,0:T(8,128)(2,1)S(1)} %get-tuple-element.10.label_ref, ...), custom_call_target="tpu_custom_call" | custom-call | tf_op jit(solution)/shard_map/closing/pallas_call | solution.py:240
  71.8 33.5 %all_to_all.10 = bf16[128,7,2,128]{3,2,1,0:T(2,128)(2,1)S(1)} all-to-all(bf16[128,7,2,128]{3,2,1,0:T(2,128)(2,1)S(1)} %bitcast.21), channel_id=1, replica_groups=mesh['y'=4,'zh'=2,'x'=4,'core'=2,'zl'=8] {'zl','y','x'}, dimensions={0} | all-to-all | bytes 917504 | tf_op jit(solution)/shard_map/all_to_all | solution.py:375
  105.3 1.3 %unpack.1 = bf16[2,216,512]{2,1,0:T(8,128)(2,1)} custom-call(bf16[1792,128]{1,0:T(8,128)(2,1)S(1)} %bitcast.22), custom_call_target="tpu_custom_call" | custom-call | tf_op jit(solution)/shard_map/unpack/pallas_call | solution.py:334
  (3 shorter events, 0.0 us)
Async XLA Ops:
  0.0 29.5 %copy-start = (bf16[2,2,216,216]{3,2,1,0:T(8,128)(2,1)S(1)}, bf16[2,2,216,216]{3,2,1,0:T(8,128)(2,1)}, u32[]{:S(2)}) copy-start(bf16[2,2,216,216]{3,2,1,0:T(8,128)(2,1)} %param.5) | copy-start | bytes 1119748
  2.3 56.7 %all-to-all-start = ((bf16[256,8,128]{2,1,0:T(8,128)(2,1)}), bf16[256,8,128]{2,1,0:T(8,128)(2,1)S(1)}, u32[]{:S(2)}, u32[]{:S(2)}) async-start(bf16[256,8,128]{2,1,0:T(8,128)(2,1)} %bitcast.23), calls=%async_computation | async-start | bytes 1048576 | tf_op jit(solution)/shard_map/all_to_all | solution.py:367
  61.8 6.3 %collective-permute-start = (bf16[256,512]{1,0:T(8,128)(2,1)S(1)}, bf16[256,512]{1,0:T(8,128)(2,1)S(1)}, u32[]{:S(2)}, u32[]{:S(2)}) collective-permute-start(bf16[256,512]{1,0:T(8,128)(2,1)S(1)} %get-tuple-element.9), channel_id=1, source_target_pairs={{0,8},{8,0},{1,9},{9,1},{2,10},{10,2},{3,11},{11,3},{4,12},{12,4},... | collective-permute-start | bytes 786440 | tf_op jit(solution)/shard_map/ppermute | solution.py:372
